TPU v7x, 32 devices: a whole 2x2x4 slice. The times are simulated.
32 devices in a mesh: row: 4 (over y, x), col: 8 (over z, core).
Axes of the slice: x: 2, y: 2, z: 4, core: 2. Of those that a mesh axis runs over, the one named last changes fastest.
Arguments:
- strips: int32 [1024, 128, 128], P(('row', 'col')), may hold values from 0 to 1073741824
- grid_pos: int32 [1024], P(('row', 'col')), may hold values from 0 to 1023, as said below
- kernel_spectra: float32 [16, 2, 1024], replicated, may hold values from -6 to 6
- weights: float32 [16], replicated, may hold values from 0.05 to 1
Outputs:
- aerial: float32 [4096, 4096], P('row', 'col')
Inputs may be any that keep to these rules, and one draw needn't show every extreme that they name: grid_pos is a permutation of 0 .. 1023; the 32 raster tiles at placement indices d * 32 .. (d + 1) * 32 - 1 lie in 32 different blocks of 1024 x 512 pixels (block (r, c) covers rows r * 1024 onward and columns c * 512 onward), one in each.
All inputs are finite; a program needn't handle non-finite values.
Results may differ from a plain program's by a relative error of at most 0.00005.
Values sent between devices are 32-bit elements; how exact they have to be, the bound alone decides.
A program may use at most 64 MiB of HBM per device.

v0:
```python
import math

import jax
import jax.numpy as jnp
from jax import lax
from jax.sharding import PartitionSpec as P

ROWS_DEV = 1024
COLS_DEV = 512
TILE = 128
KF = 32


absorber = 0.245
precise = lax.Precision.HIGHEST


def extended(block, sides, width):
    for axis, dim in sides:
        count = lax.axis_size(axis)
        forward = [(i, i + 1) for i in range(count - 1)]
        backward = [(target, source) for source, target in forward]
        low = lax.ppermute(
            lax.slice_in_dim(block, block.shape[dim] - width, None, axis=dim), axis, forward
        )
        high = lax.ppermute(lax.slice_in_dim(block, 0, width, axis=dim), axis, backward)
        block = jnp.concatenate([low, block, high], axis=dim)
    return block


def phase_table(length, offset, kept_count, window):
    position = jnp.arange(length, dtype=jnp.int32)[:, None] + offset
    half_kept = kept_count // 2
    frequency = jnp.concatenate(
        [jnp.arange(half_kept, dtype=jnp.int32), jnp.arange(half_kept, dtype=jnp.int32) - half_kept]
    )[None, :]
    phase_steps = position * frequency % window
    angles = phase_steps.astype(jnp.float32) * jnp.float32(2.0 * math.pi / window)
    return (jnp.cos(angles), jnp.sin(angles))


def aerial_tiles(spec_real, spec_imag, kernel_spectra, weights, tile_size, margin, window):
    kernel_count = kernel_spectra.shape[0]
    kept_count = spec_real.shape[1]
    kern_real = kernel_spectra[:, 0].reshape(kernel_count, kept_count, kept_count)
    kern_imag = kernel_spectra[:, 1].reshape(kernel_count, kept_count, kept_count)
    prod_real = kern_real[:, None] * spec_real[None] - kern_imag[:, None] * spec_imag[None]
    prod_imag = kern_real[:, None] * spec_imag[None] + kern_imag[:, None] * spec_real[None]
    stacked = jnp.concatenate([prod_real, prod_imag], axis=2)
    back_cos, back_sin = phase_table(tile_size, margin, kept_count, window)
    back_block = jnp.concatenate(
        [
            jnp.concatenate([back_cos, -back_sin], axis=1),
            jnp.concatenate([back_sin, back_cos], axis=1),
        ],
        axis=0,
    )
    halves = jnp.einsum("pk,nbkl->nbpl", back_block, stacked, precision=precise)
    joined = jnp.concatenate([halves[:, :, :tile_size], halves[:, :, tile_size:]], axis=3)
    out_block = jnp.concatenate(
        [
            jnp.concatenate([back_cos.T, back_sin.T], axis=1),
            jnp.concatenate([-back_sin.T, back_cos.T], axis=1),
        ],
        axis=0,
    )
    fields = jnp.einsum("nbpl,lq->nbpq", joined, out_block, precision=precise)
    field_real = fields[..., :tile_size]
    field_imag = fields[..., tile_size:]
    power = field_real * field_real + field_imag * field_imag
    return jnp.einsum("n,nbpq->bpq", weights, power, precision=precise) / jnp.float32(
        float(window) ** 4
    )


def shards(strips, grid_pos, kernel_spectra, weights):
    col_count = lax.axis_size("col")
    raster = strips.shape[1]
    block_rows = ROWS_DEV // raster
    block_cols = COLS_DEV // TILE
    raster_cols = block_cols * col_count
    strip_row = grid_pos // raster_cols
    strip_col = grid_pos % raster_cols
    owners = strip_row // block_rows * col_count + strip_col // block_cols
    slot_ids = strip_row % block_rows * block_cols + strip_col % block_cols
    send_order = jnp.argsort(owners)
    outgoing = strips[send_order]
    out_slots = slot_ids[send_order]
    received, got_slots = (
        lax.all_to_all(outgoing, ("row", "col"), split_axis=0, concat_axis=0, tiled=True),
        lax.all_to_all(out_slots, ("row", "col"), split_axis=0, concat_axis=0, tiled=True),
    )
    placing = jnp.argsort(got_slots)
    block_strips = received[placing]
    cover = (
        block_strips.reshape(block_rows, block_cols, raster, TILE)
        .transpose(0, 2, 1, 3)
        .reshape(ROWS_DEV, COLS_DEV)
    )
    transmission = 1.0 - (1.0 + absorber) * (cover.astype(jnp.float32) * jnp.float32(2.0 ** (-30)))
    padded = extended(transmission, (("row", 0), ("col", 1)), TILE // 2)
    window = 2 * TILE
    fwd_cos, fwd_sin = phase_table(window, 0, KF, window)
    row_table = jnp.concatenate([fwd_cos, -fwd_sin], axis=1)
    col_table = jnp.concatenate(
        [
            jnp.concatenate([fwd_cos.T, fwd_sin.T], axis=1),
            jnp.concatenate([-fwd_sin.T, fwd_cos.T], axis=1),
        ],
        axis=0,
    )

    def one_row(tile_row):
        row_band = lax.dynamic_slice_in_dim(padded, tile_row * TILE, window, 0)
        col_blocks = row_band.reshape(window, block_cols + 1, TILE)
        windows = jnp.concatenate([col_blocks[:, :-1], col_blocks[:, 1:]], axis=2)
        partial_value = jnp.einsum("ibj,jl->bil", windows, row_table, precision=precise)
        joined = jnp.concatenate([partial_value[:, :, :KF], partial_value[:, :, KF:]], axis=1)
        spectra = jnp.einsum("ki,bil->bkl", col_table, joined, precision=precise)
        intensity = aerial_tiles(
            spectra[:, :KF], spectra[:, KF:], kernel_spectra, weights, TILE, TILE // 2, window
        )
        return intensity.transpose(1, 0, 2).reshape(TILE, COLS_DEV)

    rows_out = lax.map(one_row, jnp.arange(ROWS_DEV // TILE, dtype=jnp.int32))
    return rows_out.reshape(ROWS_DEV, COLS_DEV)


def solution(mesh):
    return jax.shard_map(
        shards,
        mesh=mesh,
        in_specs=(P(("row", "col"), None, None), P(("row", "col")), P(), P()),
        out_specs=P("row", "col"),
        check_vma=False,
    )
```

profile of v0, /device:TPU:5, one launch (start us, length us, event | category | flops | bytes accessed | tf_op | source)
XLA Modules:
  0.0 301.8 jit_solution(3340435104008326454)
XLA Ops:
  0.9 1.6 sort.31
  3.9 6.4 %all-to-all-start.1 = ((s32[32,1,1]{2,1,0:T(1,128)}), s32[32,1,1]{2,1,0:T(1,128)S(1)}, u32[]{:S(2)}, u32[]{:S(2)}) async-start(s32[32,1,1]{2,1,0:T(1,128)} %copy.23), calls=%async_computation.1 | async-start | bytes 32768 | tf_op jit(solution)/shard_map/all_to_all | solution.py:91
  10.3 2.0 gather_fusion
  12.3 3.7 %all-to-all-done.1 = s32[32,1,1]{2,1,0:T(1,128)S(1)} async-done(((s32[32,1,1]{2,1,0:T(1,128)}), s32[32,1,1]{2,1,0:T(1,128)S(1)}, u32[]{:S(2)}, u32[]{:S(2)}) %all-to-all-start.1) | async-done | bytes 160 | tf_op jit(solution)/shard_map/all_to_all | solution.py:91
  15.9 4.8 %all-to-all-start = ((s32[32,128,128]{2,1,0:T(8,128)}), s32[32,128,128]{2,1,0:T(8,128)}, u32[]{:S(2)}, u32[]{:S(2)}) async-start(s32[32,128,128]{2,1,0:T(8,128)} %gather_fusion), calls=%async_computation | async-start | bytes 4194304 | tf_op jit(solution)/shard_map/all_to_all | solution.py:90
  21.5 1.6 sort.32
  23.1 46.9 %all-to-all-done = s32[32,128,128]{2,1,0:T(8,128)} async-done(((s32[32,128,128]{2,1,0:T(8,128)}), s32[32,128,128]{2,1,0:T(8,128)}, u32[]{:S(2)}, u32[]{:S(2)}) %all-to-all-start) | async-done | bytes 2097184 | tf_op jit(solution)/shard_map/all_to_all | solution.py:90
  70.0 3.6 %gather_fusion.2 = s32[32,128,128]{2,1,0:T(8,128)} fusion(s32[32,128,128]{2,1,0:T(8,128)} %all-to-all-done, s32[1024]{0:T(1024)S(1)} %pad_clamp_fusion), kind=kCustom, calls=%fused_computation.2 | custom fusion | bytes 4194432 | tf_op jit(solution)/shard_map/gather | solution.py:94
  73.6 3.3 %multiply_subtract_fusion.1 = f32[32,128,128]{2,1,0:T(8,128)} fusion(s32[32,128,128]{2,1,0:T(8,128)} %gather_fusion.2), kind=kLoop, calls=%fused_computation.80 | loop fusion | flops 1572864 | bytes 4194304 | tf_op jit(solution)/shard_map/sub | solution.py:100
  76.9 2.9 copy.24
  79.8 2.1 copy.37
  81.9 1.3 copy-done.1
  83.3 2.1 collective-permute-start
  85.5 4.1 %collective-permute-start.1 = (f32[64,512]{0,1:T(8,128)S(1)}, f32[64,512]{0,1:T(8,128)S(1)}, u32[]{:S(2)}, u32[]{:S(2)}) collective-permute-start(f32[64,512]{0,1:T(8,128)S(1)} %get-tuple-element.153), channel_id=1, source_target_pairs={{8,0},{16,8},{24,16},{9,1},{17,9},{25,17},{10,2},{18,10},{26,18},{... | collective-permute-start | bytes 393224 | tf_op jit(solution)/shard_map/ppermute | solution.py:26
  89.8 4.1 %collective-permute-done = f32[64,512]{0,1:T(8,128)S(1)} collective-permute-done((f32[64,512]{0,1:T(8,128)S(1)}, f32[64,512]{0,1:T(8,128)S(1)}, u32[]{:S(2)}, u32[]{:S(2)}) %collective-permute-start) | collective-permute-done | bytes 131104 | tf_op jit(solution)/shard_map/ppermute | solution.py:23
  93.9 2.6 collective-permute-done.1
  96.6 4.0 %concatenate.87 = f32[1152,512]{0,1:T(8,128)} concatenate(f32[64,512]{0,1:T(8,128)S(1)} %collective-permute-done, f32[1024,512]{0,1:T(8,128)} %bitcast.72, f32[64,512]{0,1:T(8,128)S(1)} %collective-permute-done.1), dimensions={0} | concatenate | bytes 4718592 | tf_op jit(solution)/shard_map/concatenate | solution.py:27
  101.6 1.9 collective-permute-start.2
  103.6 2.4 collective-permute-start.3
  107.2 4.4 %collective-permute-done.3 = f32[1152,64]{0,1:T(8,128)S(1)} collective-permute-done((f32[1152,64]{0,1:T(8,128)S(1)}, f32[1152,64]{0,1:T(8,128)S(1)}, u32[]{:S(2)}, u32[]{:S(2)}) %collective-permute-start.3) | collective-permute-done | bytes 294944 | tf_op jit(solution)/shard_map/ppermute | solution.py:26
  111.6 3.5 %pad_maximum_fusion = f32[1152,640]{0,1:T(8,128)} fusion(f32[1152,64]{0,1:T(8,128)S(1)} %collective-permute-done.3, f32[1152,512]{0,1:T(8,128)} %concatenate.87, f32[1152,64]{0,1:T(8,128)S(1)} %collective-permute-done.2), kind=kLoop, calls=%fused_computation.78 | loop fusion | flops 1474560 | bytes 5898240 | tf_op jit(solution)/shard_map/concatenate | solution.py:27
  115.1 186.7 %while.12 = (s32[]{:T(128)}, f32[8,128,512]{2,1,0:T(8,128)}, f32[16,2,1024]{2,1,0:T(2,128)S(1)}, s32[8]{0:T(128)S(1)}, f32[1152,640]{0,1:T(8,128)}, /*index=5*/f...) while((s32[]{:T(128)}, f32[8,128,512]{2,1,0:T(8,128)}, ...), condition=%wide.region_3.4_spmd, body=%wide.region_2.3_spmd.sunk | while | flops 2282316032 | bytes 45484912 | solution.py:125
  118.6 1.2 copy.47
  122.9 1.9 convolution_bitcast_fusion.8
  125.2 7.0 %fusion.104 = f32[16,4,128,256]{3,2,1,0:T(8,128)S(1)} fusion(f32[16,4,128,32]{2,3,1,0:T(8,128)S(1)} %get-tuple-element.240, f32[16,4,128,32]{2,3,1,0:T(8,128)S(1)} %get-tuple-element.241, f32[32,128]{1,0:T(8,128)S(1)} %get-tuple-element.242, f32[32,128]{1,0:T(8,128)S(1)} %get-tuple-element.243, f32[32,128]{1,0:T(8,128)S(1)} %get-tuple-element.244), kind=kOutput, calls=%fused_computation.8.clone.1 | convolution fusion | flops 1611186176 | bytes 10534912 | tf_op jit(solution)/shard_map/while/body/eval_jaxpr/nbpl,lq->nbpq/dot_general | solution.py:67
  132.8 4.7 %fusion.106 = f32[1,4,128,128]{3,0,2,1:T(1,128)S(1)} fusion(f32[16,4,128,128]{3,2,1,0:T(8,128)S(1)} %fusion.105, f32[16]{0:T(128)S(1)} %get-tuple-element.276), kind=kOutput, calls=%fused_computation.6.clone.1 | convolution fusion | flops 12582912 | bytes 4456512 | tf_op jit(solution)/shard_map/while/body/eval_jaxpr/n,nbpq->bpq/dot_general | solution.py:71
  141.9 1.2 copy.47
  146.2 1.9 convolution_bitcast_fusion.8
  148.5 7.0 %fusion.104 = f32[16,4,128,256]{3,2,1,0:T(8,128)S(1)} fusion(f32[16,4,128,32]{2,3,1,0:T(8,128)S(1)} %get-tuple-element.240, f32[16,4,128,32]{2,3,1,0:T(8,128)S(1)} %get-tuple-element.241, f32[32,128]{1,0:T(8,128)S(1)} %get-tuple-element.242, f32[32,128]{1,0:T(8,128)S(1)} %get-tuple-element.243, f32[32,128]{1,0:T(8,128)S(1)} %get-tuple-element.244), kind=kOutput, calls=%fused_computation.8.clone.1 | convolution fusion | flops 1611186176 | bytes 10534912 | tf_op jit(solution)/shard_map/while/body/eval_jaxpr/nbpl,lq->nbpq/dot_general | solution.py:67
  156.1 4.7 %fusion.106 = f32[1,4,128,128]{3,0,2,1:T(1,128)S(1)} fusion(f32[16,4,128,128]{3,2,1,0:T(8,128)S(1)} %fusion.105, f32[16]{0:T(128)S(1)} %get-tuple-element.276), kind=kOutput, calls=%fused_computation.6.clone.1 | convolution fusion | flops 12582912 | bytes 4456512 | tf_op jit(solution)/shard_map/while/body/eval_jaxpr/n,nbpq->bpq/dot_general | solution.py:71
  169.5 1.9 convolution_bitcast_fusion.8
  171.8 7.0 %fusion.104 = f32[16,4,128,256]{3,2,1,0:T(8,128)S(1)} fusion(f32[16,4,128,32]{2,3,1,0:T(8,128)S(1)} %get-tuple-element.240, f32[16,4,128,32]{2,3,1,0:T(8,128)S(1)} %get-tuple-element.241, f32[32,128]{1,0:T(8,128)S(1)} %get-tuple-element.242, f32[32,128]{1,0:T(8,128)S(1)} %get-tuple-element.243, f32[32,128]{1,0:T(8,128)S(1)} %get-tuple-element.244), kind=kOutput, calls=%fused_computation.8.clone.1 | convolution fusion | flops 1611186176 | bytes 10534912 | tf_op jit(solution)/shard_map/while/body/eval_jaxpr/nbpl,lq->nbpq/dot_general | solution.py:67
  179.5 4.7 %fusion.106 = f32[1,4,128,128]{3,0,2,1:T(1,128)S(1)} fusion(f32[16,4,128,128]{3,2,1,0:T(8,128)S(1)} %fusion.105, f32[16]{0:T(128)S(1)} %get-tuple-element.276), kind=kOutput, calls=%fused_computation.6.clone.1 | convolution fusion | flops 12582912 | bytes 4456512 | tf_op jit(solution)/shard_map/while/body/eval_jaxpr/n,nbpq->bpq/dot_general | solution.py:71
  192.8 1.9 convolution_bitcast_fusion.8
  195.1 7.0 %fusion.104 = f32[16,4,128,256]{3,2,1,0:T(8,128)S(1)} fusion(f32[16,4,128,32]{2,3,1,0:T(8,128)S(1)} %get-tuple-element.240, f32[16,4,128,32]{2,3,1,0:T(8,128)S(1)} %get-tuple-element.241, f32[32,128]{1,0:T(8,128)S(1)} %get-tuple-element.242, f32[32,128]{1,0:T(8,128)S(1)} %get-tuple-element.243, f32[32,128]{1,0:T(8,128)S(1)} %get-tuple-element.244), kind=kOutput, calls=%fused_computation.8.clone.1 | convolution fusion | flops 1611186176 | bytes 10534912 | tf_op jit(solution)/shard_map/while/body/eval_jaxpr/nbpl,lq->nbpq/dot_general | solution.py:67
  202.8 4.7 %fusion.106 = f32[1,4,128,128]{3,0,2,1:T(1,128)S(1)} fusion(f32[16,4,128,128]{3,2,1,0:T(8,128)S(1)} %fusion.105, f32[16]{0:T(128)S(1)} %get-tuple-element.276), kind=kOutput, calls=%fused_computation.6.clone.1 | convolution fusion | flops 12582912 | bytes 4456512 | tf_op jit(solution)/shard_map/while/body/eval_jaxpr/n,nbpq->bpq/dot_general | solution.py:71
  216.1 1.9 convolution_bitcast_fusion.8
  218.5 7.0 %fusion.104 = f32[16,4,128,256]{3,2,1,0:T(8,128)S(1)} fusion(f32[16,4,128,32]{2,3,1,0:T(8,128)S(1)} %get-tuple-element.240, f32[16,4,128,32]{2,3,1,0:T(8,128)S(1)} %get-tuple-element.241, f32[32,128]{1,0:T(8,128)S(1)} %get-tuple-element.242, f32[32,128]{1,0:T(8,128)S(1)} %get-tuple-element.243, f32[32,128]{1,0:T(8,128)S(1)} %get-tuple-element.244), kind=kOutput, calls=%fused_computation.8.clone.1 | convolution fusion | flops 1611186176 | bytes 10534912 | tf_op jit(solution)/shard_map/while/body/eval_jaxpr/nbpl,lq->nbpq/dot_general | solution.py:67
  226.1 4.7 %fusion.106 = f32[1,4,128,128]{3,0,2,1:T(1,128)S(1)} fusion(f32[16,4,128,128]{3,2,1,0:T(8,128)S(1)} %fusion.105, f32[16]{0:T(128)S(1)} %get-tuple-element.276), kind=kOutput, calls=%fused_computation.6.clone.1 | convolution fusion | flops 12582912 | bytes 4456512 | tf_op jit(solution)/shard_map/while/body/eval_jaxpr/n,nbpq->bpq/dot_general | solution.py:71
  239.4 1.9 convolution_bitcast_fusion.8
  241.8 7.0 %fusion.104 = f32[16,4,128,256]{3,2,1,0:T(8,128)S(1)} fusion(f32[16,4,128,32]{2,3,1,0:T(8,128)S(1)} %get-tuple-element.240, f32[16,4,128,32]{2,3,1,0:T(8,128)S(1)} %get-tuple-element.241, f32[32,128]{1,0:T(8,128)S(1)} %get-tuple-element.242, f32[32,128]{1,0:T(8,128)S(1)} %get-tuple-element.243, f32[32,128]{1,0:T(8,128)S(1)} %get-tuple-element.244), kind=kOutput, calls=%fused_computation.8.clone.1 | convolution fusion | flops 1611186176 | bytes 10534912 | tf_op jit(solution)/shard_map/while/body/eval_jaxpr/nbpl,lq->nbpq/dot_general | solution.py:67
  249.4 4.7 %fusion.106 = f32[1,4,128,128]{3,0,2,1:T(1,128)S(1)} fusion(f32[16,4,128,128]{3,2,1,0:T(8,128)S(1)} %fusion.105, f32[16]{0:T(128)S(1)} %get-tuple-element.276), kind=kOutput, calls=%fused_computation.6.clone.1 | convolution fusion | flops 12582912 | bytes 4456512 | tf_op jit(solution)/shard_map/while/body/eval_jaxpr/n,nbpq->bpq/dot_general | solution.py:71
  262.7 1.9 convolution_bitcast_fusion.8
  265.1 7.0 %fusion.104 = f32[16,4,128,256]{3,2,1,0:T(8,128)S(1)} fusion(f32[16,4,128,32]{2,3,1,0:T(8,128)S(1)} %get-tuple-element.240, f32[16,4,128,32]{2,3,1,0:T(8,128)S(1)} %get-tuple-element.241, f32[32,128]{1,0:T(8,128)S(1)} %get-tuple-element.242, f32[32,128]{1,0:T(8,128)S(1)} %get-tuple-element.243, f32[32,128]{1,0:T(8,128)S(1)} %get-tuple-element.244), kind=kOutput, calls=%fused_computation.8.clone.1 | convolution fusion | flops 1611186176 | bytes 10534912 | tf_op jit(solution)/shard_map/while/body/eval_jaxpr/nbpl,lq->nbpq/dot_general | solution.py:67
  272.7 4.7 %fusion.106 = f32[1,4,128,128]{3,0,2,1:T(1,128)S(1)} fusion(f32[16,4,128,128]{3,2,1,0:T(8,128)S(1)} %fusion.105, f32[16]{0:T(128)S(1)} %get-tuple-element.276), kind=kOutput, calls=%fused_computation.6.clone.1 | convolution fusion | flops 12582912 | bytes 4456512 | tf_op jit(solution)/shard_map/while/body/eval_jaxpr/n,nbpq->bpq/dot_general | solution.py:71
  286.1 1.9 convolution_bitcast_fusion.8
  288.4 7.0 %fusion.104 = f32[16,4,128,256]{3,2,1,0:T(8,128)S(1)} fusion(f32[16,4,128,32]{2,3,1,0:T(8,128)S(1)} %get-tuple-element.240, f32[16,4,128,32]{2,3,1,0:T(8,128)S(1)} %get-tuple-element.241, f32[32,128]{1,0:T(8,128)S(1)} %get-tuple-element.242, f32[32,128]{1,0:T(8,128)S(1)} %get-tuple-element.243, f32[32,128]{1,0:T(8,128)S(1)} %get-tuple-element.244), kind=kOutput, calls=%fused_computation.8.clone.1 | convolution fusion | flops 1611186176 | bytes 10534912 | tf_op jit(solution)/shard_map/while/body/eval_jaxpr/nbpl,lq->nbpq/dot_general | solution.py:67
  296.0 4.7 %fusion.106 = f32[1,4,128,128]{3,0,2,1:T(1,128)S(1)} fusion(f32[16,4,128,128]{3,2,1,0:T(8,128)S(1)} %fusion.105, f32[16]{0:T(128)S(1)} %get-tuple-element.276), kind=kOutput, calls=%fused_computation.6.clone.1 | convolution fusion | flops 12582912 | bytes 4456512 | tf_op jit(solution)/shard_map/while/body/eval_jaxpr/n,nbpq->bpq/dot_general | solution.py:71
  (236 shorter events, 75.7 us)
Async XLA Ops:
  0.0 10.3 %copy-start = (s32[32,128,128]{2,1,0:T(8,128)S(1)}, s32[32,128,128]{2,1,0:T(8,128)}, u32[]{:S(2)}) copy-start(s32[32,128,128]{2,1,0:T(8,128)} %param.6) | copy-start | bytes 6291460
  3.9 12.1 %all-to-all-start.1 = ((s32[32,1,1]{2,1,0:T(1,128)}), s32[32,1,1]{2,1,0:T(1,128)S(1)}, u32[]{:S(2)}, u32[]{:S(2)}) async-start(s32[32,1,1]{2,1,0:T(1,128)} %copy.23), calls=%async_computation.1 | async-start | bytes 32768 | tf_op jit(solution)/shard_map/all_to_all | solution.py:91
  15.9 54.0 %all-to-all-start = ((s32[32,128,128]{2,1,0:T(8,128)}), s32[32,128,128]{2,1,0:T(8,128)}, u32[]{:S(2)}, u32[]{:S(2)}) async-start(s32[32,128,128]{2,1,0:T(8,128)} %gather_fusion), calls=%async_computation | async-start | bytes 4194304 | tf_op jit(solution)/shard_map/all_to_all | solution.py:90
  81.9 1.3 copy-start.1
  83.3 10.6 %collective-permute-start = (f32[64,512]{0,1:T(8,128)S(1)}, f32[64,512]{0,1:T(8,128)S(1)}, u32[]{:S(2)}, u32[]{:S(2)}) collective-permute-start(f32[64,512]{0,1:T(8,128)S(1)} %get-tuple-element.154), channel_id=1, source_target_pairs={{0,8},{8,16},{16,24},{1,9},{9,17},{17,25},{2,10},{10,18},{18,26},{... | collective-permute-start | bytes 393224 | tf_op jit(solution)/shard_map/ppermute | solution.py:23
  85.5 11.1 %collective-permute-start.1 = (f32[64,512]{0,1:T(8,128)S(1)}, f32[64,512]{0,1:T(8,128)S(1)}, u32[]{:S(2)}, u32[]{:S(2)}) collective-permute-start(f32[64,512]{0,1:T(8,128)S(1)} %get-tuple-element.153), channel_id=1, source_target_pairs={{8,0},{16,8},{24,16},{9,1},{17,9},{25,17},{10,2},{18,10},{26,18},{... | collective-permute-start | bytes 393224 | tf_op jit(solution)/shard_map/ppermute | solution.py:26
  101.6 5.6 %collective-permute-start.2 = (f32[1152,64]{0,1:T(8,128)S(1)}, f32[1152,64]{0,1:T(8,128)S(1)}, u32[]{:S(2)}, u32[]{:S(2)}) collective-permute-start(f32[1152,64]{0,1:T(8,128)S(1)} %get-tuple-element.151), channel_id=1, source_target_pairs={{0,1},{1,2},{2,3},{3,4},{4,5},{5,6},{6,7},{8,9},{9,10},{10,11},{11... | collective-permute-start | bytes 884744 | tf_op jit(solution)/shard_map/ppermute | solution.py:23
  103.6 8.0 %collective-permute-start.3 = (f32[1152,64]{0,1:T(8,128)S(1)}, f32[1152,64]{0,1:T(8,128)S(1)}, u32[]{:S(2)}, u32[]{:S(2)}) collective-permute-start(f32[1152,64]{0,1:T(8,128)S(1)} %get-tuple-element.152), channel_id=1, source_target_pairs={{1,0},{2,1},{3,2},{4,3},{5,4},{6,5},{7,6},{9,8},{10,9},{11,10},{12... | collective-permute-start | bytes 884744 | tf_op jit(solution)/shard_map/ppermute | solution.py:26
  106.2 8.8 %copy-start.2 = (f32[16,2,1024]{2,1,0:T(2,128)S(1)}, f32[16,2,1024]{2,1,0:T(2,128)}, u32[]{:S(2)}) copy-start(f32[16,2,1024]{2,1,0:T(2,128)} %param.8) | copy-start | bytes 393220
  106.2 8.8 %copy-start.3 = (f32[16]{0:T(128)S(1)}, f32[16]{0:T(128)}, u32[]{:S(2)}) copy-start(f32[16]{0:T(128)} %param.9) | copy-start | bytes 196
where the time goes:
time: 307 us; the launch traced here: 302 us
  matrix products  120 us (39%)
  local copies, waits for them, and re-layouts  66.9 us (22%)
  waiting for transfers between devices  62.7 us (20%)
  other arithmetic  24.2 us (8%)
  starting transfers between devices  21.7 us (7%)
  loops' own time  5.79 us (2%)
    dot_general x8, matrix products, aerial_tiles(): fields = jnp.einsum('nbpl,lq->nbpq', joined, out_block, precision=precise)  55.8 us
    all_to_all x1, waiting for transfers between devices, shards(): lax.all_to_all(outgoing, ('row', 'col'), split_axis=0, concat_axis=0, til...  46.9 us
    dot_general x8, matrix products, aerial_tiles(): jnp.einsum('n,nbpq->bpq', weights, power, precision=precise)  37.4 us
    dot_general x8, matrix products, aerial_tiles(): halves = jnp.einsum('pk,nbkl->nbpl', back_block, stacked, precision=precise)  15.1 us
    while x16, local copies, waits for them, and re-layouts  11.4 us
    dot_general x8, matrix products, one_row(): jnp.einsum('ibj,jl->bil', windows, row_table, precision=precise)  9.11 us
    dynamic_slice x8, local copies, waits for them, and re-layouts, one_row(): row_band = lax.dynamic_slice_in_dim(padded, tile_row * TILE, window, 0)  9.09 us
    slice x8, local copies, waits for them, and re-layouts, one_row(): windows = jnp.concatenate([col_blocks[:, :-1], col_blocks[:, 1:]], axis=2)  7.12 us
  transfers between devices with their start and end apart: 6, of which 6 were waited for; matrix products, arithmetic and copies ran while one was open for 2% of the time, Pallas kernels for 0%

commit v1 on v0

v1 whole, which is shorter than its diff:
```python
import functools

import jax
import jax.numpy as jnp
import numpy as np
from jax import lax
from jax.experimental import pallas as pl
from jax.experimental.pallas import tpu as pltpu
from jax.sharding import PartitionSpec as P

ROWS_DEV = 1024
COLS_DEV = 512
TILE = 128
KF = 32
HALO = TILE // 2
WIN = 2 * TILE
COARSE = 2 * KF
GROUP = 4

absorber = 0.245
bf16 = jnp.bfloat16
f32 = jnp.float32


def halves_of(table):
    high = table.astype(np.float32).astype(bf16)
    low = (table - high.astype(np.float64)).astype(np.float32).astype(bf16)
    return high, low


def frequencies():
    return np.concatenate([np.arange(KF // 2), np.arange(KF // 2) - KF // 2])


def cos_sin(positions):
    angle = 2.0 * np.pi / WIN * ((positions[:, None] * frequencies()[None, :]) % WIN)
    return np.cos(angle), np.sin(angle)


@functools.cache
def tables():
    fwd_cos, fwd_sin = cos_sin(np.arange(WIN))
    col = np.concatenate([np.tile(fwd_cos, (1, GROUP)), np.tile(-fwd_sin, (1, GROUP))], axis=1)
    row = np.block([[fwd_cos.T, fwd_sin.T], [-fwd_sin.T, fwd_cos.T]])
    c, s = cos_sin(np.arange(COARSE) * (WIN // COARSE))
    up = np.block([[c, -s], [s, c]])
    eye = np.eye(GROUP)
    kc, ks = np.kron(eye, c.T), np.kron(eye, s.T)
    across = np.block([[kc, ks], [-ks, kc]])
    shift = (np.arange(TILE) + HALO)[:, None] - (WIN // COARSE) * np.arange(COARSE)[None, :]
    orders = np.arange(1 - KF, KF)
    fine = np.cos(2.0 * np.pi / WIN * ((shift[:, :, None] * orders) % WIN)).sum(-1) / COARSE
    col_hi, col_lo = halves_of(col)
    row_hi, row_lo = halves_of(row)
    up_hi, up_lo = halves_of(up)
    across_hi, across_lo = halves_of(across)
    wide_hi, wide_lo = halves_of(np.tile(fine.T, (GROUP, 1)))
    fine_hi, fine_lo = halves_of(fine)
    return (
        col_hi,
        col_lo,
        row_hi,
        row_lo,
        np.concatenate([up_hi, up_hi, up_lo], axis=1),
        across_hi,
        across_lo,
        wide_hi,
        wide_lo,
        np.concatenate([fine_hi, fine_hi, fine_lo], axis=1),
    )


def mm(a, b):
    return jnp.dot(a, b, preferred_element_type=f32)


def split(x):
    high = x.astype(bf16)
    return high, (x - high.astype(f32)).astype(bf16)


def transmitted(cover):
    return 1.0 - (1.0 + absorber) * (cover.astype(f32) * jnp.float32(2.0 ** (-30)))


def image_kernel(
    place,
    recv,
    top,
    bottom,
    left,
    right,
    kern,
    col_hi,
    col_lo,
    row_hi,
    row_lo,
    up,
    across_hi,
    across_lo,
    wide_hi,
    wide_lo,
    fine,
    out,
    padded,
):
    raster = recv.shape[1] - 8
    block_cols = out.shape[1] // TILE
    block_rows = recv.shape[0] // block_cols
    rows, cols = padded.shape
    step = pl.program_id(0)

    @pl.when(step == 0)
    def _():
        padded[:HALO, HALO : cols - HALO] = top[...]
        padded[rows - HALO :, HALO : cols - HALO] = bottom[...]
        padded[:, :HALO] = left[...]
        padded[:, cols - HALO :] = right[...]

        @pl.loop(0, block_rows)
        def _(i):
            for j in range(block_cols):
                cover = recv[place[i * block_cols + j], :raster, :]
                padded[
                    pl.ds(pl.multiple_of(HALO + i * raster, 8), raster),
                    HALO + j * TILE : HALO + (j + 1) * TILE,
                ] = transmitted(cover)

    first = pl.multiple_of(step * TILE, TILE)
    lanes = GROUP * KF
    groups = kern.shape[2] // lanes
    for j in range(block_cols):
        window = padded[pl.ds(first, WIN), j * TILE : j * TILE + WIN]
        hi, lo = split(window)
        part = mm(hi, col_hi[...]) + mm(lo, col_hi[...]) + mm(hi, col_lo[...])
        part = jnp.concatenate([part[:, :lanes], part[:, lanes:]], axis=0)
        hi, lo = split(part)
        spec = mm(row_hi[...], hi) + mm(row_hi[...], lo) + mm(row_lo[...], hi)
        spec_re = jnp.concatenate([spec[:KF]] * groups, axis=1)
        spec_im = jnp.concatenate([spec[KF:]] * groups, axis=1)
        prod = jnp.concatenate(
            [kern[0] * spec_re - kern[1] * spec_im, kern[0] * spec_im + kern[1] * spec_re], axis=0
        )
        hi, lo = split(prod)
        half = mm(up[...], jnp.concatenate([hi, lo, hi], axis=0))
        half = jnp.concatenate(
            [
                jnp.concatenate(
                    [
                        half[:COARSE, g * lanes : (g + 1) * lanes],
                        half[COARSE:, g * lanes : (g + 1) * lanes],
                    ],
                    axis=1,
                )
                for g in range(groups)
            ],
            axis=0,
        )
        hi, lo = split(half)
        field = mm(hi, across_hi[...]) + mm(lo, across_hi[...]) + mm(hi, across_lo[...])
        wide = field.shape[1] // 2
        power = field[:, :wide] * field[:, :wide] + field[:, wide:] * field[:, wide:]
        power = sum(power[g * COARSE : (g + 1) * COARSE] for g in range(groups))
        hi, lo = split(power)
        power = mm(hi, wide_hi[...]) + mm(lo, wide_hi[...]) + mm(hi, wide_lo[...])
        hi, lo = split(power)
        out[:, j * TILE : (j + 1) * TILE] = mm(fine[...], jnp.concatenate([hi, lo, hi], axis=0))


def image(place, recv, top, bottom, left, right, kern):
    full = lambda shape: pl.BlockSpec(shape, lambda i: (0,) * len(shape))
    whole = [recv, top, bottom, left, right, kern, *(jnp.asarray(t) for t in tables())]
    return pl.pallas_call(
        image_kernel,
        grid=(ROWS_DEV // TILE,),
        in_specs=[pl.BlockSpec(memory_space=pltpu.SMEM)] + [full(a.shape) for a in whole],
        out_specs=pl.BlockSpec((TILE, COLS_DEV), lambda i: (i, 0)),
        out_shape=jax.ShapeDtypeStruct((ROWS_DEV, COLS_DEV), f32),
        scratch_shapes=[pltpu.VMEM((ROWS_DEV + 2 * HALO, COLS_DEV + 2 * HALO), f32)],
        name="image",
    )(place, *whole)


def swap(low_side, high_side, axis):
    count = lax.axis_size(axis)
    forward = [(i, i + 1) for i in range(count - 1)]
    backward = [(i + 1, i) for i in range(count - 1)]
    return lax.ppermute(high_side, axis, forward), lax.ppermute(low_side, axis, backward)


def inverse(keys):
    count = keys.shape[0]
    ids = jnp.arange(count, dtype=jnp.int32)
    return jnp.sum(jnp.where(keys[None, :] == ids[:, None], ids[None, :], 0), axis=1)


def shards(strips, grid_pos, kernel_spectra, weights):
    col_count = lax.axis_size("col")
    count, raster = strips.shape[:2]
    block_rows = ROWS_DEV // raster
    block_cols = COLS_DEV // TILE
    raster_cols = block_cols * col_count
    strip_row = grid_pos // raster_cols
    strip_col = grid_pos % raster_cols
    owners = strip_row // block_rows * col_count + strip_col // block_cols
    slot_ids = strip_row % block_rows * block_cols + strip_col % block_cols
    order = inverse(owners)
    tagged = jnp.concatenate(
        [strips, jnp.broadcast_to(slot_ids[:, None, None], (count, 8, TILE))], axis=1
    )
    received = lax.all_to_all(
        tagged[order], ("row", "col"), split_axis=0, concat_axis=0, tiled=True
    )
    place = inverse(received[:, raster, 0])
    grid = place.reshape(block_rows, block_cols)
    edge_rows = HALO // raster if raster < HALO else 1

    def row_edge(ids, start):
        part = received[ids.reshape(-1), start : start + min(raster, HALO)]
        part = part.reshape(edge_rows, block_cols, -1, TILE).transpose(0, 2, 1, 3)
        return transmitted(part.reshape(HALO, COLS_DEV))

    def col_edge(ids, start):
        return transmitted(received[ids, :raster, start : start + HALO].reshape(ROWS_DEV, HALO))

    top, bottom = swap(
        row_edge(grid[:edge_rows], 0), row_edge(grid[-edge_rows:], max(raster - HALO, 0)), "row"
    )
    left, right = swap(
        jnp.concatenate([top[:, :HALO], col_edge(grid[:, 0], 0), bottom[:, :HALO]], axis=0),
        jnp.concatenate(
            [top[:, -HALO:], col_edge(grid[:, -1], TILE - HALO), bottom[:, -HALO:]], axis=0
        ),
        "col",
    )
    kernels = kernel_spectra.shape[0]
    scale = jnp.sqrt(weights) * jnp.float32(1.0 / WIN**2)
    kern = kernel_spectra.reshape(kernels, 2, KF, KF) * scale[:, None, None, None]
    kern = kern.transpose(1, 2, 0, 3).reshape(2, KF, kernels * KF)
    return image(place, received, top, bottom, left, right, kern)


def solution(mesh):
    return jax.shard_map(
        shards,
        mesh=mesh,
        in_specs=(P(("row", "col"), None, None), P(("row", "col")), P(), P()),
        out_specs=P("row", "col"),
        check_vma=False,
    )
```

time: 307 us -> 181 us (0.59); the launches traced: 302 us -> 180 us
  matrix products: 120 us -> 0 us
  Pallas kernels: 0 us -> 41.8 us
  other arithmetic: 24.2 us -> 3.45 us
  local copies, waits for them, and re-layouts: 66.9 us -> 58.8 us
  loops' own time: 5.79 us -> 0.44 us
  starting transfers between devices: 21.7 us -> 16.7 us
  waiting for transfers between devices: 62.7 us -> 58.6 us
    dot_general x40 -> x0, matrix products: 120 us -> none  [the longest x8 55.8 us: aerial_tiles(): fields = jnp.einsum('nbpl,lq->nbpq', joined, out_block, precision=precise)]
    pallas_call x0 -> x1, Pallas kernels: none -> 41.8 us  [image(): pl.pallas_call(image_kernel, grid=(ROWS_DEV // TILE,), in_specs=[pl.Block...]
    gather x3 -> x51, local copies, waits for them, and re-layouts: 6.29 us -> 47.4 us  [the longest x1 3.59 us: shards(): block_strips = received[placing]]
    dynamic_slice x16 -> x0, local copies, waits for them, and re-layouts: 13.5 us -> none  [the longest x8 9.09 us: one_row(): row_band = lax.dynamic_slice_in_dim(padded, tile_row * TILE, window, 0)]
    slice x42 -> x7, local copies, waits for them, and re-layouts: 14.1 us -> 1.13 us  [the longest x1 0.68 us: shards(): place = inverse(received[:, raster, 0])]
    while x16 -> x0, local copies, waits for them, and re-layouts: 11.4 us -> none
    dynamic_update_slice x8 -> x0, local copies, waits for them, and re-layouts: 5.81 us -> none  [shards(): rows_out = lax.map(one_row, jnp.arange(ROWS_DEV // TILE, dtype=jnp.int32))]
    sub x18 -> x4, other arithmetic: 5.7 us -> 0.21 us  [transmitted(): 1.0 - (1.0 + absorber) * (cover.astype(f32) * jnp.float32(2.0 ** (-30)))]
  transfers between devices with their start and end apart: 6 -> 5, of which waited for: 6 -> 4; matrix products, arithmetic and copies ran while one was open for 2% -> 3% of each run, Pallas kernels for 0% -> 0%
where the time goes in v1:
time: 181 us; the launch traced here: 180 us
  local copies, waits for them, and re-layouts  58.8 us (32%)
  waiting for transfers between devices  58.6 us (32%)
  Pallas kernels  41.8 us (23%)
  starting transfers between devices  16.7 us (9%)
  other arithmetic  3.45 us (2%)
    all_to_all x1, waiting for transfers between devices, shards(): lax.all_to_all(tagged[order], ('row', 'col'), split_axis=0, concat_axis=0...  51.8 us
    gather x48, local copies, waits for them, and re-layouts  42.1 us
    pallas_call x1, Pallas kernels, image(): pl.pallas_call(image_kernel, grid=(ROWS_DEV // TILE,), in_specs=[pl.Block...  41.8 us
    ppermute x2, starting transfers between devices, swap(): lax.ppermute(low_side, axis, backward)  6.38 us
    all_to_all x1, starting transfers between devices, shards(): lax.all_to_all(tagged[order], ('row', 'col'), split_axis=0, concat_axis=0...  6.38 us
    ppermute x2, waiting for transfers between devices, swap(): lax.ppermute(high_side, axis, forward)  4.45 us
    ppermute x2, starting transfers between devices, swap(): lax.ppermute(high_side, axis, forward)  3.92 us
  transfers between devices with their start and end apart: 5, of which 4 were waited for; matrix products, arithmetic and copies ran while one was open for 3% of the time, Pallas kernels for 0%

profile of v1, /device:TPU:5, one launch (start us, length us, event | category | flops | bytes accessed | tf_op | source)
XLA Modules:
  0.0 180.0 jit_solution(12283839502601125574)
XLA Ops:
  0.0 0.7 multiply_add_fusion
  0.9 1.8 pad_add_fusion
  2.7 2.1 %gather_fusion = s32[32,136,128]{2,1,0:T(8,128)} fusion(s32[32,136,128]{2,1,0:T(8,128)S(1)} %pad_add_fusion, s32[1024]{0:T(1024)S(1)} %pad_clamp_fusion), kind=kCustom, calls=%fused_computation | custom fusion | bytes 4456576 | tf_op jit(solution)/shard_map/gather | solution.py:212
  4.8 6.4 %all-to-all-start = ((s32[32,136,128]{2,1,0:T(8,128)}), s32[32,136,128]{2,1,0:T(8,128)S(1)}, u32[]{:S(2)}, u32[]{:S(2)}) async-start(s32[32,136,128]{2,1,0:T(8,128)} %gather_fusion), calls=%async_computation | async-start | bytes 4456448 | tf_op jit(solution)/shard_map/all_to_all | solution.py:211
  11.2 51.8 %all-to-all-done.recv = s32[32,136,128]{2,1,0:T(8,128)S(1)} async-done(((s32[32,136,128]{2,1,0:T(8,128)}), s32[32,136,128]{2,1,0:T(8,128)S(1)}, u32[]{:S(2)}, u32[]{:S(2)}) %all-to-all-start) | async-done | bytes 2228256 | tf_op jit(solution)/shard_map/all_to_all | solution.py:211
  63.1 0.7 slice_reduce_fusion
  64.1 21.3 %while.3 = (s32[]{:T(128)}, s32[32,136,128]{2,1,0:T(8,128)S(1)}, s32[8,3]{1,0:T(8,128)S(1)}, s32[8,128,64]{2,1,0:T(8,128)S(1)}, s32[]{:T(128)}) while((s32[]{:T(128)}, s32[32,136,128]{2,1,0:T(8,128)S(1)}, s32[8,3]{1,0:T(8,128)S(1)}, s32[8,128,64]{2,1,0:T(8,128)S(1)}, s32[]{:T(128)}) %tuple.52), condition=%wide.while_cond.1, body=%wide.while_body.1.sunk | while | flops 2 | bytes 131209 | solution.py:224
  64.2 0.6 fusion.16
  64.8 2.0 %dynamic-slice_dynamic-update-slice_fusion.5 = s32[8,128,64]{2,1,0:T(8,128)S(1)} fusion(s32[8,128,64]{2,1,0:T(8,128)S(1)} %get-tuple-element.171, s32[]{:T(128)S(6)} %copy.80, s32[32,136,128]{2,1,0:T(8,128)S(1)} %get-tuple-element.174, s32[]{:T(128)} %bitcast.54, s32[]{:T(128)} %bitcast.55, s32[]{:T(128)} %bitcast.56), kind=kLoop, calls=%fused_computation.5.clone.1 | loop fusion | bytes 131088 | tf_op jit(solution)/shard_map/gather
  66.8 0.6 fusion.16
  67.5 2.0 %dynamic-slice_dynamic-update-slice_fusion.5 = s32[8,128,64]{2,1,0:T(8,128)S(1)} fusion(s32[8,128,64]{2,1,0:T(8,128)S(1)} %get-tuple-element.171, s32[]{:T(128)S(6)} %copy.80, s32[32,136,128]{2,1,0:T(8,128)S(1)} %get-tuple-element.174, s32[]{:T(128)} %bitcast.54, s32[]{:T(128)} %bitcast.55, s32[]{:T(128)} %bitcast.56), kind=kLoop, calls=%fused_computation.5.clone.1 | loop fusion | bytes 131088 | tf_op jit(solution)/shard_map/gather
  69.5 0.6 fusion.16
  70.1 2.0 %dynamic-slice_dynamic-update-slice_fusion.5 = s32[8,128,64]{2,1,0:T(8,128)S(1)} fusion(s32[8,128,64]{2,1,0:T(8,128)S(1)} %get-tuple-element.171, s32[]{:T(128)S(6)} %copy.80, s32[32,136,128]{2,1,0:T(8,128)S(1)} %get-tuple-element.174, s32[]{:T(128)} %bitcast.54, s32[]{:T(128)} %bitcast.55, s32[]{:T(128)} %bitcast.56), kind=kLoop, calls=%fused_computation.5.clone.1 | loop fusion | bytes 131088 | tf_op jit(solution)/shard_map/gather
  72.2 0.6 fusion.16
  72.8 2.0 %dynamic-slice_dynamic-update-slice_fusion.5 = s32[8,128,64]{2,1,0:T(8,128)S(1)} fusion(s32[8,128,64]{2,1,0:T(8,128)S(1)} %get-tuple-element.171, s32[]{:T(128)S(6)} %copy.80, s32[32,136,128]{2,1,0:T(8,128)S(1)} %get-tuple-element.174, s32[]{:T(128)} %bitcast.54, s32[]{:T(128)} %bitcast.55, s32[]{:T(128)} %bitcast.56), kind=kLoop, calls=%fused_computation.5.clone.1 | loop fusion | bytes 131088 | tf_op jit(solution)/shard_map/gather
  74.8 0.6 fusion.16
  75.5 2.0 %dynamic-slice_dynamic-update-slice_fusion.5 = s32[8,128,64]{2,1,0:T(8,128)S(1)} fusion(s32[8,128,64]{2,1,0:T(8,128)S(1)} %get-tuple-element.171, s32[]{:T(128)S(6)} %copy.80, s32[32,136,128]{2,1,0:T(8,128)S(1)} %get-tuple-element.174, s32[]{:T(128)} %bitcast.54, s32[]{:T(128)} %bitcast.55, s32[]{:T(128)} %bitcast.56), kind=kLoop, calls=%fused_computation.5.clone.1 | loop fusion | bytes 131088 | tf_op jit(solution)/shard_map/gather
  78.1 2.0 %dynamic-slice_dynamic-update-slice_fusion.5 = s32[8,128,64]{2,1,0:T(8,128)S(1)} fusion(s32[8,128,64]{2,1,0:T(8,128)S(1)} %get-tuple-element.171, s32[]{:T(128)S(6)} %copy.80, s32[32,136,128]{2,1,0:T(8,128)S(1)} %get-tuple-element.174, s32[]{:T(128)} %bitcast.54, s32[]{:T(128)} %bitcast.55, s32[]{:T(128)} %bitcast.56), kind=kLoop, calls=%fused_computation.5.clone.1 | loop fusion | bytes 131088 | tf_op jit(solution)/shard_map/gather
  80.1 0.6 fusion.16
  80.8 2.0 %dynamic-slice_dynamic-update-slice_fusion.5 = s32[8,128,64]{2,1,0:T(8,128)S(1)} fusion(s32[8,128,64]{2,1,0:T(8,128)S(1)} %get-tuple-element.171, s32[]{:T(128)S(6)} %copy.80, s32[32,136,128]{2,1,0:T(8,128)S(1)} %get-tuple-element.174, s32[]{:T(128)} %bitcast.54, s32[]{:T(128)} %bitcast.55, s32[]{:T(128)} %bitcast.56), kind=kLoop, calls=%fused_computation.5.clone.1 | loop fusion | bytes 131088 | tf_op jit(solution)/shard_map/gather
  82.8 0.6 fusion.16
  83.4 2.0 %dynamic-slice_dynamic-update-slice_fusion.5 = s32[8,128,64]{2,1,0:T(8,128)S(1)} fusion(s32[8,128,64]{2,1,0:T(8,128)S(1)} %get-tuple-element.171, s32[]{:T(128)S(6)} %copy.80, s32[32,136,128]{2,1,0:T(8,128)S(1)} %get-tuple-element.174, s32[]{:T(128)} %bitcast.54, s32[]{:T(128)} %bitcast.55, s32[]{:T(128)} %bitcast.56), kind=kLoop, calls=%fused_computation.5.clone.1 | loop fusion | bytes 131088 | tf_op jit(solution)/shard_map/gather
  85.8 21.3 %while.2 = (s32[]{:T(128)}, s32[32,136,128]{2,1,0:T(8,128)S(1)}, s32[8,3]{1,0:T(8,128)S(1)}, s32[8,128,64]{2,1,0:T(8,128)S(1)}, s32[]{:T(128)}) while((s32[]{:T(128)}, s32[32,136,128]{2,1,0:T(8,128)S(1)}, s32[8,3]{1,0:T(8,128)S(1)}, s32[8,128,64]{2,1,0:T(8,128)S(1)}, s32[]{:T(128)}) %tuple.55), condition=%wide.while_cond, body=%wide.while_body.sunk | while | flops 2 | bytes 131209 | solution.py:224
  86.5 2.0 %dynamic-slice_dynamic-update-slice_fusion.4 = s32[8,128,64]{2,1,0:T(8,128)S(1)} fusion(s32[8,128,64]{2,1,0:T(8,128)S(1)} %get-tuple-element.156, s32[]{:T(128)S(6)} %copy.74, s32[32,136,128]{2,1,0:T(8,128)S(1)} %get-tuple-element.159, s32[]{:T(128)} %bitcast.51, s32[]{:T(128)} %bitcast.52, s32[]{:T(128)} %bitcast.53), kind=kLoop, calls=%fused_computation.3.clone.1 | loop fusion | bytes 131088 | tf_op jit(solution)/shard_map/gather
  89.1 2.0 %dynamic-slice_dynamic-update-slice_fusion.4 = s32[8,128,64]{2,1,0:T(8,128)S(1)} fusion(s32[8,128,64]{2,1,0:T(8,128)S(1)} %get-tuple-element.156, s32[]{:T(128)S(6)} %copy.74, s32[32,136,128]{2,1,0:T(8,128)S(1)} %get-tuple-element.159, s32[]{:T(128)} %bitcast.51, s32[]{:T(128)} %bitcast.52, s32[]{:T(128)} %bitcast.53), kind=kLoop, calls=%fused_computation.3.clone.1 | loop fusion | bytes 131088 | tf_op jit(solution)/shard_map/gather
  91.8 2.0 %dynamic-slice_dynamic-update-slice_fusion.4 = s32[8,128,64]{2,1,0:T(8,128)S(1)} fusion(s32[8,128,64]{2,1,0:T(8,128)S(1)} %get-tuple-element.156, s32[]{:T(128)S(6)} %copy.74, s32[32,136,128]{2,1,0:T(8,128)S(1)} %get-tuple-element.159, s32[]{:T(128)} %bitcast.51, s32[]{:T(128)} %bitcast.52, s32[]{:T(128)} %bitcast.53), kind=kLoop, calls=%fused_computation.3.clone.1 | loop fusion | bytes 131088 | tf_op jit(solution)/shard_map/gather
  94.5 2.0 %dynamic-slice_dynamic-update-slice_fusion.4 = s32[8,128,64]{2,1,0:T(8,128)S(1)} fusion(s32[8,128,64]{2,1,0:T(8,128)S(1)} %get-tuple-element.156, s32[]{:T(128)S(6)} %copy.74, s32[32,136,128]{2,1,0:T(8,128)S(1)} %get-tuple-element.159, s32[]{:T(128)} %bitcast.51, s32[]{:T(128)} %bitcast.52, s32[]{:T(128)} %bitcast.53), kind=kLoop, calls=%fused_computation.3.clone.1 | loop fusion | bytes 131088 | tf_op jit(solution)/shard_map/gather
  97.1 2.0 %dynamic-slice_dynamic-update-slice_fusion.4 = s32[8,128,64]{2,1,0:T(8,128)S(1)} fusion(s32[8,128,64]{2,1,0:T(8,128)S(1)} %get-tuple-element.156, s32[]{:T(128)S(6)} %copy.74, s32[32,136,128]{2,1,0:T(8,128)S(1)} %get-tuple-element.159, s32[]{:T(128)} %bitcast.51, s32[]{:T(128)} %bitcast.52, s32[]{:T(128)} %bitcast.53), kind=kLoop, calls=%fused_computation.3.clone.1 | loop fusion | bytes 131088 | tf_op jit(solution)/shard_map/gather
  99.8 2.0 %dynamic-slice_dynamic-update-slice_fusion.4 = s32[8,128,64]{2,1,0:T(8,128)S(1)} fusion(s32[8,128,64]{2,1,0:T(8,128)S(1)} %get-tuple-element.156, s32[]{:T(128)S(6)} %copy.74, s32[32,136,128]{2,1,0:T(8,128)S(1)} %get-tuple-element.159, s32[]{:T(128)} %bitcast.51, s32[]{:T(128)} %bitcast.52, s32[]{:T(128)} %bitcast.53), kind=kLoop, calls=%fused_computation.3.clone.1 | loop fusion | bytes 131088 | tf_op jit(solution)/shard_map/gather
  102.4 2.0 %dynamic-slice_dynamic-update-slice_fusion.4 = s32[8,128,64]{2,1,0:T(8,128)S(1)} fusion(s32[8,128,64]{2,1,0:T(8,128)S(1)} %get-tuple-element.156, s32[]{:T(128)S(6)} %copy.74, s32[32,136,128]{2,1,0:T(8,128)S(1)} %get-tuple-element.159, s32[]{:T(128)} %bitcast.51, s32[]{:T(128)} %bitcast.52, s32[]{:T(128)} %bitcast.53), kind=kLoop, calls=%fused_computation.3.clone.1 | loop fusion | bytes 131088 | tf_op jit(solution)/shard_map/gather
  105.1 2.0 %dynamic-slice_dynamic-update-slice_fusion.4 = s32[8,128,64]{2,1,0:T(8,128)S(1)} fusion(s32[8,128,64]{2,1,0:T(8,128)S(1)} %get-tuple-element.156, s32[]{:T(128)S(6)} %copy.74, s32[32,136,128]{2,1,0:T(8,128)S(1)} %get-tuple-element.159, s32[]{:T(128)} %bitcast.51, s32[]{:T(128)} %bitcast.52, s32[]{:T(128)} %bitcast.53), kind=kLoop, calls=%fused_computation.3.clone.1 | loop fusion | bytes 131088 | tf_op jit(solution)/shard_map/gather
  107.3 1.8 copy.38
  109.1 1.6 gather_fusion.2
  110.7 1.6 gather_fusion.1
  112.4 3.3 %collective-permute-start.1 = (f32[64,512]{1,0:T(8,128)S(1)}, f32[64,512]{1,0:T(8,128)S(1)}, u32[]{:S(2)}, u32[]{:S(2)}) collective-permute-start(f32[64,512]{1,0:T(8,128)S(1)} %bitcast.62), channel_id=1, source_target_pairs={{8,0},{16,8},{24,16},{9,1},{17,9},{25,17},{10,2},{18,10},{26,18},{... | collective-permute-start | bytes 393224 | tf_op jit(solution)/shard_map/ppermute | solution.py:188
  115.8 2.0 %collective-permute-start = (f32[64,512]{1,0:T(8,128)S(1)}, f32[64,512]{1,0:T(8,128)S(1)}, u32[]{:S(2)}, u32[]{:S(2)}) collective-permute-start(f32[64,512]{1,0:T(8,128)S(1)} %bitcast.61), channel_id=1, source_target_pairs={{0,8},{8,16},{16,24},{1,9},{9,17},{17,25},{2,10},{10,18},{18,26},{... | collective-permute-start | bytes 393224 | tf_op jit(solution)/shard_map/ppermute | solution.py:188
  117.8 1.5 collective-permute-done.1.bottom
  119.5 4.4 %collective-permute-done.top = f32[64,512]{1,0:T(8,128)S(1)} collective-permute-done((f32[64,512]{1,0:T(8,128)S(1)}, f32[64,512]{1,0:T(8,128)S(1)}, u32[]{:S(2)}, u32[]{:S(2)}) %collective-permute-start) | collective-permute-done | bytes 131104 | tf_op jit(solution)/shard_map/ppermute | solution.py:188
  124.2 0.9 concatenate.25
  125.1 1.9 %collective-permute-start.2 = (f32[1152,64]{0,1:T(8,128)}, f32[1152,64]{0,1:T(8,128)}, u32[]{:S(2)}, u32[]{:S(2)}) collective-permute-start(f32[1152,64]{0,1:T(8,128)} %concatenate.25), channel_id=1, source_target_pairs={{0,1},{1,2},{2,3},{3,4},{4,5},{5,6},{6,7},{8,9},{9,10},{10,11},{11... | collective-permute-start | bytes 884744 | tf_op jit(solution)/shard_map/ppermute | solution.py:188
  127.0 0.9 concatenate.27
  127.9 3.1 %collective-permute-start.3 = (f32[1152,64]{0,1:T(8,128)}, f32[1152,64]{0,1:T(8,128)}, u32[]{:S(2)}, u32[]{:S(2)}) collective-permute-start(f32[1152,64]{0,1:T(8,128)} %concatenate.27), channel_id=1, source_target_pairs={{1,0},{2,1},{3,2},{4,3},{5,4},{6,5},{7,6},{9,8},{10,9},{11,10},{12... | collective-permute-start | bytes 884744 | tf_op jit(solution)/shard_map/ppermute | solution.py:188
  131.0 1.1 reshape.65
  132.5 0.9 reshape.66.kern
  133.4 2.0 %copy.49.left = f32[1152,64]{1,0:T(8,128)} copy(f32[1152,64]{0,1:T(8,128)} %collective-permute-done.2) | data formatting | bytes 589824 | tf_op jit(solution)/shard_map/ppermute | solution.py:188
  135.4 0.8 collective-permute-done.3
  136.2 2.0 %copy.50.right = f32[1152,64]{1,0:T(8,128)} copy(f32[1152,64]{0,1:T(8,128)} %collective-permute-done.3) | data formatting | bytes 589824 | tf_op jit(solution)/shard_map/ppermute | solution.py:188
  138.2 41.8 %image.1 = f32[1024,512]{1,0:T(8,128)} custom-call(s32[32]{0:T(128)} %copy-done.2, s32[32,136,128]{2,1,0:T(8,128)S(1)} %get-tuple-element.180, f32[64,512]{1,0:T(8,128)} %copy-done.1, f32[64,512]{1,0:T(8,128)} %copy-done, f32[1152,64]{1,0:T(8,128)} %copy.49.left, f32[1152,64]{1,0:T(8,128)} %copy.50.right, f32[2,32,512]{2,1,0:T(8,128)} %reshape.66.kern, ...), custom_call_target="tpu_custom_call" | custom-call | tf_op jit(solution)/shard_map/image/pallas_call | solution.py:173
  (65 shorter events, 8.1 us)
Async XLA Ops:
  4.8 58.3 %all-to-all-start = ((s32[32,136,128]{2,1,0:T(8,128)}), s32[32,136,128]{2,1,0:T(8,128)S(1)}, u32[]{:S(2)}, u32[]{:S(2)}) async-start(s32[32,136,128]{2,1,0:T(8,128)} %gather_fusion), calls=%async_computation | async-start | bytes 4456448 | tf_op jit(solution)/shard_map/all_to_all | solution.py:211
  63.9 21.9 %copy-start.2 = (s32[32]{0:T(128)}, s32[32]{0:T(128)S(1)}, u32[]{:S(2)}) copy-start(s32[32]{0:T(128)S(1)} %select_reduce_fusion.place) | copy-start | bytes 388
  110.7 20.3 %copy-start.3 = (f32[16]{0:T(128)S(1)}, f32[16]{0:T(128)}, u32[]{:S(2)}) copy-start(f32[16]{0:T(128)} %param.17) | copy-start | bytes 196
  112.4 6.9 %collective-permute-start.1 = (f32[64,512]{1,0:T(8,128)S(1)}, f32[64,512]{1,0:T(8,128)S(1)}, u32[]{:S(2)}, u32[]{:S(2)}) collective-permute-start(f32[64,512]{1,0:T(8,128)S(1)} %bitcast.62), channel_id=1, source_target_pairs={{8,0},{16,8},{24,16},{9,1},{17,9},{25,17},{10,2},{18,10},{26,18},{... | collective-permute-start | bytes 393224 | tf_op jit(solution)/shard_map/ppermute | solution.py:188
  115.8 8.2 %collective-permute-start = (f32[64,512]{1,0:T(8,128)S(1)}, f32[64,512]{1,0:T(8,128)S(1)}, u32[]{:S(2)}, u32[]{:S(2)}) collective-permute-start(f32[64,512]{1,0:T(8,128)S(1)} %bitcast.61), channel_id=1, source_target_pairs={{0,8},{8,16},{16,24},{1,9},{9,17},{17,25},{2,10},{10,18},{18,26},{... | collective-permute-start | bytes 393224 | tf_op jit(solution)/shard_map/ppermute | solution.py:188
  119.3 11.7 %copy-start = (f32[64,512]{1,0:T(8,128)}, f32[64,512]{1,0:T(8,128)S(1)}, u32[]{:S(2)}) copy-start(f32[64,512]{1,0:T(8,128)S(1)} %collective-permute-done.1.bottom) | copy-start | bytes 393220
  124.0 7.0 %copy-start.1 = (f32[64,512]{1,0:T(8,128)}, f32[64,512]{1,0:T(8,128)S(1)}, u32[]{:S(2)}) copy-start(f32[64,512]{1,0:T(8,128)S(1)} %collective-permute-done.top) | copy-start | bytes 393220
  125.1 8.3 %collective-permute-start.2 = (f32[1152,64]{0,1:T(8,128)}, f32[1152,64]{0,1:T(8,128)}, u32[]{:S(2)}, u32[]{:S(2)}) collective-permute-start(f32[1152,64]{0,1:T(8,128)} %concatenate.25), channel_id=1, source_target_pairs={{0,1},{1,2},{2,3},{3,4},{4,5},{5,6},{6,7},{8,9},{9,10},{10,11},{11... | collective-permute-start | bytes 884744 | tf_op jit(solution)/shard_map/ppermute | solution.py:188
  127.9 8.3 %collective-permute-start.3 = (f32[1152,64]{0,1:T(8,128)}, f32[1152,64]{0,1:T(8,128)}, u32[]{:S(2)}, u32[]{:S(2)}) collective-permute-start(f32[1152,64]{0,1:T(8,128)} %concatenate.27), channel_id=1, source_target_pairs={{1,0},{2,1},{3,2},{4,3},{5,4},{6,5},{7,6},{9,8},{10,9},{11,10},{12... | collective-permute-start | bytes 884744 | tf_op jit(solution)/shard_map/ppermute | solution.py:188

commit v2 on v1

v2 whole, which is shorter than its diff:
```python
import functools
import math

import jax
import jax.numpy as jnp
import numpy as np
from jax import lax
from jax.experimental import pallas as pl
from jax.experimental.pallas import tpu as pltpu
from jax.sharding import PartitionSpec as P

ROWS_DEV = 1024
COLS_DEV = 512
TILE = 128
KF = 32
HALO = TILE // 2
WIN = 2 * TILE
COARSE = 2 * KF
GROUP = 4

absorber = 0.245
bf16 = jnp.bfloat16
f32 = jnp.float32


def halves_of(table):
    high = table.astype(np.float32).astype(bf16)
    low = (table - high.astype(np.float64)).astype(np.float32).astype(bf16)
    return high, low


def frequencies():
    return np.concatenate([np.arange(KF // 2), np.arange(KF // 2) - KF // 2])


def cos_sin(positions):
    angle = 2.0 * np.pi / WIN * ((positions[:, None] * frequencies()[None, :]) % WIN)
    return np.cos(angle), np.sin(angle)


def sums_of(length):
    if length < HALO:
        return np.eye(length)
    x = np.arange(length) - (length - 1) / 2
    angle = 2.0 * np.pi / WIN * np.arange(KF // 2 + 1)[:, None] * x[None, :]
    return np.concatenate([np.cos(angle), np.sin(angle[1:])])


def phases_of(length):
    k = frequencies()
    first = np.arange(WIN // length) * length
    if length < HALO:
        place = first[:, None] + np.arange(length)[None, :]
        return np.exp(-2j * np.pi / WIN * (k[:, None, None] * place[None] % WIN))
    centre = first + (length - 1) / 2
    turn = np.exp(-2j * np.pi / WIN * k[:, None] * centre[None, :])
    pick = np.zeros((KF, KF + 1), complex)
    for i, f in enumerate(k):
        pick[i, abs(f)] = 1.0
        if f != 0:
            pick[i, KF // 2 + abs(f)] = -1j * np.sign(f)
    return turn[:, :, None] * pick[:, None, :]


def sent_rows(length):
    return -(-(sums_of(length).shape[0] + 3) // 8) * 8


@functools.cache
def pack_tables(raster):
    length = min(raster, HALO)
    parts = raster // length
    row = sums_of(length)
    count, rows = row.shape[0], sent_rows(length)
    across = np.kron(np.eye(2), sums_of(HALO)).reshape(2, KF + 1, TILE)
    main = across[:, :KF].reshape(2 * KF, TILE).T
    main = np.concatenate([main] * parts + [np.zeros((TILE, TILE - parts * 2 * KF))], axis=1)
    extra = np.zeros((rows, TILE))
    extra[count : count + 2] = across[:, KF]
    down = np.zeros((rows, raster))
    down[:count] = np.tile(row, (1, parts))
    turned = np.zeros((raster, TILE))
    for p in range(parts):
        turned[p * length : (p + 1) * length, p * 2 * KF : p * 2 * KF + count] = row.T
    return (*halves_of(main), *halves_of(extra), *halves_of(down), *halves_of(turned))


@functools.cache
def tables(raster):
    length = min(raster, HALO)
    parts = raster // length
    count, rows = sums_of(length).shape[0], sent_rows(length)
    phase = phases_of(HALO)
    lanes = GROUP * KF
    main = np.zeros((3, TILE, parts, 2, GROUP, KF))
    extra = np.zeros((3, 8, 2, GROUP, KF))
    for segment, (tile, half) in enumerate([(0, 1), (1, 0), (1, 1), (2, 0)]):
        for ri, value in enumerate([phase[:, segment].real, phase[:, segment].imag]):
            for p in range(parts):
                at = p * 2 * KF + half * KF
                main[tile, at : at + KF, p, ri] = value.T[:KF, None, :]
            extra[tile, count % 8 + half, ri] = value.T[KF, None, :]
    main = main.reshape(3 * TILE, parts * 2 * lanes)
    extra = extra.reshape(24, 2 * lanes)
    down = np.zeros((KF, WIN // length, rows), complex)
    down[:, :, :count] = phases_of(length)
    down = down.reshape(KF, -1)
    row = np.block([[down.real, -down.imag], [down.imag, down.real]])
    c, s = cos_sin(np.arange(COARSE) * (WIN // COARSE))
    up = np.block([[c, -s], [s, c]])
    eye = np.eye(GROUP)
    kc, ks = np.kron(eye, c.T), np.kron(eye, s.T)
    across = np.block([[kc, ks], [-ks, kc]])
    shift = (np.arange(TILE) + HALO)[:, None] - (WIN // COARSE) * np.arange(COARSE)[None, :]
    orders = np.arange(1 - KF, KF)
    fine = np.cos(2.0 * np.pi / WIN * ((shift[:, :, None] * orders) % WIN)).sum(-1) / COARSE
    up_hi, up_lo = halves_of(up)
    fine_hi, fine_lo = halves_of(fine)
    return (
        *halves_of(main),
        *halves_of(extra),
        *halves_of(row),
        np.concatenate([up_hi, up_hi, up_lo], axis=1),
        *halves_of(across),
        *halves_of(np.tile(fine.T, (GROUP, 1))),
        np.concatenate([fine_hi, fine_hi, fine_lo], axis=1),
    )


def mm(a, b):
    return jnp.dot(a, b, preferred_element_type=f32)


def split(x):
    high = x.astype(bf16)
    return high, (x - high.astype(f32)).astype(bf16)


def dot3(a, b, dims=((1,), (0,))):
    dot = lambda x, y: lax.dot_general(x, y, (dims, ((), ())), preferred_element_type=f32)
    return dot(a[0], b[0]) + dot(a[1], b[0]) + dot(a[0], b[1])


def transmitted(cover):
    return 1.0 - (1.0 + absorber) * (cover.astype(f32) * jnp.float32(2.0 ** (-30)))


def pack_kernel(
    order,
    slots,
    strips,
    main_hi,
    main_lo,
    extra_hi,
    extra_lo,
    down_hi,
    down_lo,
    turned_hi,
    turned_lo,
    out,
):
    count, rows, _ = out.shape
    raster = strips.shape[1]
    length = min(raster, HALO)
    sums = sums_of(length).shape[0]
    batch = math.gcd(count, 8)
    row_part = lax.broadcasted_iota(jnp.int32, (raster, TILE), 0) // length
    lane_part = lax.broadcasted_iota(jnp.int32, (raster, TILE), 1) // (2 * KF)
    keep = row_part == lane_part
    slot_row = lax.broadcasted_iota(jnp.int32, (rows, TILE), 0) == sums + 2
    main, extra = (main_hi[...], main_lo[...]), (extra_hi[...], extra_lo[...])
    down, turned = (down_hi[...], down_lo[...]), (turned_hi[...], turned_lo[...])

    @pl.loop(0, count // batch)
    def _(i):
        for j in range(batch):
            at = i * batch + j
            pixels = split(transmitted(strips[order[at]]))
            wide = jnp.where(keep, dot3(pixels, main), 0.0)
            sent = dot3(down, split(wide))
            turn = dot3(extra, pixels, ((1,), (1,)))
            sent = sent + dot3(split(turn), turned)
            out[at] = jnp.where(slot_row, slots[at], sent)


def pack(order, slots, strips):
    count, raster, _ = strips.shape
    consts = [jnp.asarray(t) for t in pack_tables(raster)]
    smem, vmem = pl.BlockSpec(memory_space=pltpu.SMEM), pl.BlockSpec(memory_space=pltpu.VMEM)
    return pl.pallas_call(
        pack_kernel,
        in_specs=[smem, smem] + [vmem] * (1 + len(consts)),
        out_specs=vmem,
        out_shape=jax.ShapeDtypeStruct((count, sent_rows(min(raster, HALO)), TILE), f32),
        name="pack",
    )(order, slots, strips, *consts)


def image_kernel(
    raster,
    place,
    recv,
    top,
    bottom,
    left,
    right,
    kern,
    main_hi,
    main_lo,
    extra_hi,
    extra_lo,
    row_hi,
    row_lo,
    up,
    across_hi,
    across_lo,
    wide_hi,
    wide_lo,
    fine,
    out,
    sums,
    partial,
):
    length = min(raster, HALO)
    parts = raster // length
    kept = sums_of(length).shape[0]
    rows = recv.shape[1]
    block_cols = out.shape[1] // TILE
    block_rows = recv.shape[0] // block_cols
    edge = top.shape[0] // block_cols
    ext_rows = block_rows + 2 * edge
    step = pl.program_id(0)
    lanes = GROUP * KF

    @pl.when(step == 0)
    def _():
        @pl.loop(0, block_rows)
        def _(i):
            for j in range(block_cols):
                at = pl.ds(pl.multiple_of((i + edge) * rows, 8), rows)
                sums[at, (j + 1) * TILE : (j + 2) * TILE] = recv[place[i * block_cols + j]]

        for i in range(edge):
            for j in range(block_cols):
                at = slice((j + 1) * TILE, (j + 2) * TILE)
                sums[i * rows : (i + 1) * rows, at] = top[i * block_cols + j]
                k = ext_rows - edge + i
                sums[k * rows : (k + 1) * rows, at] = bottom[i * block_cols + j]

        main, extra = (main_hi[...], main_lo[...]), (extra_hi[...], extra_lo[...])

        @pl.loop(0, ext_rows)
        def _(i):
            at = pl.ds(pl.multiple_of(i * rows, 8), rows)
            sums[at, :TILE] = left[i]
            sums[at, (block_cols + 1) * TILE :] = right[i]

        @pl.loop(0, ext_rows)
        def _(i):
            at = pl.ds(pl.multiple_of(i * rows, 8), rows)
            for j in range(block_cols):
                tiles = sums[at, j * TILE : (j + 3) * TILE]
                got = dot3(split(tiles), main)
                first = kept // 8 * 8
                ends = jnp.concatenate(
                    [tiles[first : first + 8, t * TILE : (t + 1) * TILE] for t in range(3)], axis=0
                )
                more = dot3(split(ends), extra, ((0,), (0,)))
                for p in range(parts):
                    to = pl.multiple_of((i * parts + p) * rows, 8)
                    partial[j, pl.ds(to, rows), :] = (
                        got[:, p * 2 * lanes : (p + 1) * 2 * lanes]
                        + more[p * 2 * KF : p * 2 * KF + rows]
                    )

    first = pl.multiple_of(
        (step * (TILE // length) + edge * parts - HALO // length) * rows, 8
    )
    groups = kern.shape[2] // lanes
    for j in range(block_cols):
        part = partial[j, pl.ds(first, WIN // length * rows), :]
        part = jnp.concatenate([part[:, :lanes], part[:, lanes:]], axis=0)
        hi, lo = split(part)
        spec = mm(row_hi[...], hi) + mm(row_hi[...], lo) + mm(row_lo[...], hi)
        spec_re = jnp.concatenate([spec[:KF]] * groups, axis=1)
        spec_im = jnp.concatenate([spec[KF:]] * groups, axis=1)
        prod = jnp.concatenate(
            [kern[0] * spec_re - kern[1] * spec_im, kern[0] * spec_im + kern[1] * spec_re], axis=0
        )
        hi, lo = split(prod)
        half = mm(up[...], jnp.concatenate([hi, lo, hi], axis=0))
        half = jnp.concatenate(
            [
                jnp.concatenate(
                    [
                        half[:COARSE, g * lanes : (g + 1) * lanes],
                        half[COARSE:, g * lanes : (g + 1) * lanes],
                    ],
                    axis=1,
                )
                for g in range(groups)
            ],
            axis=0,
        )
        hi, lo = split(half)
        field = mm(hi, across_hi[...]) + mm(lo, across_hi[...]) + mm(hi, across_lo[...])
        wide = field.shape[1] // 2
        power = field[:, :wide] * field[:, :wide] + field[:, wide:] * field[:, wide:]
        power = sum(power[g * COARSE : (g + 1) * COARSE] for g in range(groups))
        hi, lo = split(power)
        power = mm(hi, wide_hi[...]) + mm(lo, wide_hi[...]) + mm(hi, wide_lo[...])
        hi, lo = split(power)
        out[:, j * TILE : (j + 1) * TILE] = mm(fine[...], jnp.concatenate([hi, lo, hi], axis=0))


def image(raster, place, recv, top, bottom, left, right, kern):
    full = lambda shape: pl.BlockSpec(shape, lambda i: (0,) * len(shape))
    consts = [jnp.asarray(t) for t in tables(raster)]
    whole = [recv, top, bottom, left, right, kern, *consts]
    block_cols = COLS_DEV // TILE
    ext_rows, rows, _ = left.shape
    parts = max(raster // HALO, 1)
    return pl.pallas_call(
        functools.partial(image_kernel, raster),
        grid=(ROWS_DEV // TILE,),
        in_specs=[pl.BlockSpec(memory_space=pltpu.SMEM)] + [full(a.shape) for a in whole],
        out_specs=pl.BlockSpec((TILE, COLS_DEV), lambda i: (i, 0)),
        out_shape=jax.ShapeDtypeStruct((ROWS_DEV, COLS_DEV), f32),
        scratch_shapes=[
            pltpu.VMEM((ext_rows * rows, (block_cols + 2) * TILE), f32),
            pltpu.VMEM((block_cols, ext_rows * parts * rows, 2 * GROUP * KF), f32),
        ],
        name="image",
    )(place, *whole)


def swap(low_side, high_side, axis):
    count = lax.axis_size(axis)
    forward = [(i, i + 1) for i in range(count - 1)]
    backward = [(i + 1, i) for i in range(count - 1)]
    return lax.ppermute(high_side, axis, forward), lax.ppermute(low_side, axis, backward)


def inverse(keys):
    count = keys.shape[0]
    ids = jnp.arange(count, dtype=jnp.int32)
    return jnp.sum(jnp.where(keys[None, :] == ids[:, None], ids[None, :], 0), axis=1)


def shards(strips, grid_pos, kernel_spectra, weights):
    col_count = lax.axis_size("col")
    count, raster = strips.shape[:2]
    block_rows = ROWS_DEV // raster
    block_cols = COLS_DEV // TILE
    raster_cols = block_cols * col_count
    strip_row = grid_pos // raster_cols
    strip_col = grid_pos % raster_cols
    owners = strip_row // block_rows * col_count + strip_col // block_cols
    slot_ids = strip_row % block_rows * block_cols + strip_col % block_cols
    order = inverse(owners)
    sent = pack(order, slot_ids.astype(f32)[order], strips)
    received = lax.all_to_all(sent, ("row", "col"), split_axis=0, concat_axis=0, tiled=True)
    slot_row = sums_of(min(raster, HALO)).shape[0] + 2
    place = inverse(received[:, slot_row, 0].astype(jnp.int32))
    grid = place.reshape(block_rows, block_cols)
    edge = max(HALO // raster, 1)
    top, bottom = swap(
        received[grid[:edge].reshape(-1)], received[grid[-edge:].reshape(-1)], "row"
    )
    left, right = swap(
        jnp.concatenate([top[::block_cols], received[grid[:, 0]], bottom[::block_cols]]),
        jnp.concatenate(
            [
                top[block_cols - 1 :: block_cols],
                received[grid[:, -1]],
                bottom[block_cols - 1 :: block_cols],
            ]
        ),
        "col",
    )
    kernels = kernel_spectra.shape[0]
    scale = jnp.sqrt(weights) * jnp.float32(1.0 / WIN**2)
    kern = kernel_spectra.reshape(kernels, 2, KF, KF) * scale[:, None, None, None]
    kern = kern.transpose(1, 2, 0, 3).reshape(2, KF, kernels * KF)
    return image(raster, place, received, top, bottom, left, right, kern)


def solution(mesh):
    return jax.shard_map(
        shards,
        mesh=mesh,
        in_specs=(P(("row", "col"), None, None), P(("row", "col")), P(), P()),
        out_specs=P("row", "col"),
        check_vma=False,
    )
```

time: 181 us -> 105 us (0.58)
  local copies, waits for them, and re-layouts: 58.8 us -> 5.34 us
  waiting for transfers between devices: 58.6 us -> 25.3 us
  Pallas kernels: 41.8 us -> 55.2 us
    gather x51 -> x5, local copies, waits for them, and re-layouts: 47.4 us -> 3.44 us  [the longest x1 1.2 us: shards(): sent = pack(order, slot_ids.astype(f32)[order], strips)]
    all_to_all x1, waiting for transfers between devices: 51.8 us -> 17.8 us  [shards(): lax.all_to_all(sent, ('row', 'col'), split_axis=0, concat_axis=0, tiled=T...]
    pallas_call x1 -> x2, Pallas kernels: 41.8 us -> 55.2 us  [the longest x1 42.3 us: image(): pl.pallas_call(functools.partial(image_kernel, raster), grid=(ROWS_DEV //...]
    ppermute x2 -> x0, local copies, waits for them, and re-layouts: 4.03 us -> none  [the longest x1 2.02 us: swap(): lax.ppermute(low_side, axis, backward)]
    concatenate x3 -> x2, other arithmetic: 1.92 us -> 0.03 us  [the longest x1 0.02 us: shards(): jnp.concatenate([top[::block_cols], received[grid[:, 0]], bottom[::block_...]
    concatenate x4 -> x0, local copies, waits for them, and re-layouts: 1.83 us -> none  [the longest x1 0.88 us: shards(): jnp.concatenate([top[:, -HALO:], col_edge(grid[:, -1], TILE - HALO), bott...]
  transfers between devices with their start and end apart: 5 -> 5, of which waited for: 4 -> 3; matrix products, arithmetic and copies ran while one was open for 3% -> 3% of each run, Pallas kernels for 0% -> 0%
where the time goes in v2:
time: 105 us; the launch traced here: 104 us
  Pallas kernels  55.2 us (53%)
  waiting for transfers between devices  25.3 us (24%)
  starting transfers between devices  16 us (15%)
  local copies, waits for them, and re-layouts  5.34 us (5%)
  other arithmetic  2.2 us (2%)
    pallas_call x1, Pallas kernels, image(): pl.pallas_call(functools.partial(image_kernel, raster), grid=(ROWS_DEV //...  42.3 us
    all_to_all x1, waiting for transfers between devices, shards(): lax.all_to_all(sent, ('row', 'col'), split_axis=0, concat_axis=0, tiled=T...  17.8 us
    pallas_call x1, Pallas kernels, pack(): pl.pallas_call(pack_kernel, in_specs=[smem, smem] + [vmem] * (1 + len(con...  12.9 us
    all_to_all x1, starting transfers between devices, shards(): lax.all_to_all(sent, ('row', 'col'), split_axis=0, concat_axis=0, tiled=T...  6.38 us
    ppermute x2, starting transfers between devices, swap(): lax.ppermute(low_side, axis, backward)  5.26 us
    ppermute x2, starting transfers between devices, swap(): lax.ppermute(high_side, axis, forward)  4.36 us
    ppermute x2, waiting for transfers between devices, swap(): lax.ppermute(low_side, axis, backward)  3.71 us
    ppermute x2, waiting for transfers between devices, swap(): lax.ppermute(high_side, axis, forward)  3.71 us
  transfers between devices with their start and end apart: 5, of which 3 were waited for; matrix products, arithmetic and copies ran while one was open for 3% of the time, Pallas kernels for 0%

profile of v2, /device:TPU:5, one launch (start us, length us, event | category | flops | bytes accessed | tf_op | source)
XLA Modules:
  0.0 104.2 jit_solution(12800584281040688931)
XLA Ops:
  0.0 0.7 fusion.7
  0.7 0.1 select_reduce_fusion.1.order
  0.8 0.0 copy-start.7
  0.8 1.2 %gather_fusion = f32[32]{0:T(128)} fusion(f32[32]{0:T(128)S(1)} %get-tuple-element.7, s32[1024]{0:T(1024)S(1)} %pad_clamp_fusion.4), kind=kCustom, calls=%fused_computation | custom fusion | bytes 384 | tf_op jit(solution)/shard_map/gather | solution.py:361
  2.0 0.0 copy-done.7
  2.0 0.0 copy-start.5
  2.0 0.0 copy-start.8
  2.0 12.9 %pack.1 = f32[32,40,128]{2,1,0:T(8,128)} custom-call(s32[32]{0:T(128)} %copy-done.7, f32[32]{0:T(128)} %gather_fusion, s32[32,128,128]{2,1,0:T(8,128)} %strips.1, bf16[128,128]{1,0:T(8,128)(2,1)} %constant.118.clone.main_hi, bf16[128,128]{1,0:T(8,128)(2,1)} %constant.119.clone.main_lo, bf16[40,128]{1,0:T(8,128)(2,1)} %constant.120.clone.extra_hi, ...), custom_call_target="tpu_custom_call" | custom-call | tf_op jit(solution)/shard_map/pack/pallas_call | solution.py:190
  15.0 6.4 %all-to-all-start = ((f32[32,40,128]{2,1,0:T(8,128)}), f32[32,40,128]{2,1,0:T(8,128)S(1)}, u32[]{:S(2)}, u32[]{:S(2)}) async-start(f32[32,40,128]{2,1,0:T(8,128)} %pack.1), calls=%async_computation | async-start | bytes 1310720 | tf_op jit(solution)/shard_map/all_to_all | solution.py:362
  21.4 0.0 copy-done.5
  21.4 0.2 reshape.37
  21.6 0.0 copy-done.8
  21.7 17.8 %all-to-all-done.recv = f32[32,40,128]{2,1,0:T(8,128)S(1)} async-done(((f32[32,40,128]{2,1,0:T(8,128)}), f32[32,40,128]{2,1,0:T(8,128)S(1)}, u32[]{:S(2)}, u32[]{:S(2)}) %all-to-all-start) | async-done | bytes 655392 | tf_op jit(solution)/shard_map/all_to_all | solution.py:362
  39.5 0.0 copy-start
  39.5 0.7 fusion.1
  40.2 0.1 select_reduce_fusion.place
  40.3 0.0 copy-start.6
  40.3 0.1 compare_select_fusion.2
  40.4 0.1 reshape.36
  40.5 0.2 fusion.3
  40.6 0.6 gather_fusion.2
  41.2 3.1 %collective-permute-start.1 = (f32[4,40,128]{2,1,0:T(8,128)S(1)}, f32[4,40,128]{2,1,0:T(8,128)S(1)}, u32[]{:S(2)}, u32[]{:S(2)}) collective-permute-start(f32[4,40,128]{2,1,0:T(8,128)S(1)} %gather_fusion.2), channel_id=1, source_target_pairs={{8,0},{16,8},{24,16},{9,1},{17,9},{25,17},{10,2},{18,10},{26,18},{... | collective-permute-start | bytes 245768 | tf_op jit(solution)/shard_map/ppermute | solution.py:341
  44.3 0.6 gather_fusion.1
  44.9 2.2 %collective-permute-start = (f32[4,40,128]{2,1,0:T(8,128)S(1)}, f32[4,40,128]{2,1,0:T(8,128)S(1)}, u32[]{:S(2)}, u32[]{:S(2)}) collective-permute-start(f32[4,40,128]{2,1,0:T(8,128)S(1)} %gather_fusion.1), channel_id=1, source_target_pairs={{0,8},{8,16},{16,24},{1,9},{9,17},{17,25},{2,10},{10,18},{18,26},{... | collective-permute-start | bytes 245768 | tf_op jit(solution)/shard_map/ppermute | solution.py:341
  47.1 0.6 gather_fusion.4
  47.7 0.6 gather_fusion.3
  48.2 0.0 collective-permute-done.1.bottom
  48.2 0.0 copy-start.3
  48.3 3.7 %collective-permute-done.top = f32[4,40,128]{2,1,0:T(8,128)S(1)} collective-permute-done((f32[4,40,128]{2,1,0:T(8,128)S(1)}, f32[4,40,128]{2,1,0:T(8,128)S(1)}, u32[]{:S(2)}, u32[]{:S(2)}) %collective-permute-start) | collective-permute-done | bytes 81952 | tf_op jit(solution)/shard_map/ppermute | solution.py:341
  52.0 0.0 copy-start.4
  52.0 2.2 %collective-permute-start.2 = (f32[10,40,128]{2,1,0:T(8,128)S(1)}, f32[10,40,128]{2,1,0:T(8,128)S(1)}, u32[]{:S(2)}, u32[]{:S(2)}) collective-permute-start(f32[10,40,128]{2,1,0:T(8,128)S(1)} %pad_maximum_fusion), channel_id=1, source_target_pairs={{0,1},{1,2},{2,3},{3,4},{4,5},{5,6},{6,7},{8,9},{9,10},{10,11},{11... | collective-permute-start | bytes 614408 | tf_op jit(solution)/shard_map/ppermute | solution.py:341
  54.2 2.2 %collective-permute-start.3 = (f32[10,40,128]{2,1,0:T(8,128)S(1)}, f32[10,40,128]{2,1,0:T(8,128)S(1)}, u32[]{:S(2)}, u32[]{:S(2)}) collective-permute-start(f32[10,40,128]{2,1,0:T(8,128)S(1)} %pad_maximum_fusion.1), channel_id=1, source_target_pairs={{1,0},{2,1},{3,2},{4,3},{5,4},{6,5},{7,6},{9,8},{10,9},{11,10},{12... | collective-permute-start | bytes 614408 | tf_op jit(solution)/shard_map/ppermute | solution.py:341
  56.4 0.3 fusion
  56.7 0.9 reshape.38.kern
  57.6 0.0 collective-permute-done.2.left
  57.6 0.0 copy-start.1
  57.6 3.7 %collective-permute-done.3.right = f32[10,40,128]{2,1,0:T(8,128)S(1)} collective-permute-done((f32[10,40,128]{2,1,0:T(8,128)S(1)}, f32[10,40,128]{2,1,0:T(8,128)S(1)}, u32[]{:S(2)}, u32[]{:S(2)}) %collective-permute-start.3) | collective-permute-done | bytes 204832 | tf_op jit(solution)/shard_map/ppermute | solution.py:341
  61.3 0.0 copy-done
  61.3 0.0 copy-done.6
  61.3 0.0 copy-done.3
  61.3 0.0 copy-done.4
  61.3 0.0 copy-done.1
  61.3 0.0 copy-start.2
  61.3 0.7 copy-done.2
  62.0 42.3 %image.1 = f32[1024,512]{1,0:T(8,128)} custom-call(s32[32]{0:T(128)} %copy-done.6, f32[32,40,128]{2,1,0:T(8,128)} %copy-done, f32[4,40,128]{2,1,0:T(8,128)} %copy-done.4, f32[4,40,128]{2,1,0:T(8,128)} %copy-done.3, f32[10,40,128]{2,1,0:T(8,128)} %copy-done.1, f32[10,40,128]{2,1,0:T(8,128)} %copy-done.2, f32[2,32,512]{2,1,0:T(8,128)} %reshape.38.kern, ...), custom_call_target="tpu_custom_call" | custom-call | tf_op jit(solution)/shard_map/image/pallas_call | solution.py:323
  (11 shorter events, 0.1 us)
Async XLA Ops:
  0.8 1.2 %copy-start.7 = (s32[32]{0:T(128)}, s32[32]{0:T(128)S(1)}, u32[]{:S(2)}) copy-start(s32[32]{0:T(128)S(1)} %select_reduce_fusion.1.order) | copy-start | bytes 388
  2.0 19.3 %copy-start.5 = (f32[16,2,1024]{2,1,0:T(2,128)S(1)}, f32[16,2,1024]{2,1,0:T(2,128)}, u32[]{:S(2)}) copy-start(f32[16,2,1024]{2,1,0:T(2,128)} %param.26) | copy-start | bytes 393220
  2.0 19.6 %copy-start.8 = (f32[16]{0:T(128)S(1)}, f32[16]{0:T(128)}, u32[]{:S(2)}) copy-start(f32[16]{0:T(128)} %param.27) | copy-start | bytes 196
  15.0 24.5 %all-to-all-start = ((f32[32,40,128]{2,1,0:T(8,128)}), f32[32,40,128]{2,1,0:T(8,128)S(1)}, u32[]{:S(2)}, u32[]{:S(2)}) async-start(f32[32,40,128]{2,1,0:T(8,128)} %pack.1), calls=%async_computation | async-start | bytes 1310720 | tf_op jit(solution)/shard_map/all_to_all | solution.py:362
  39.5 21.8 %copy-start = (f32[32,40,128]{2,1,0:T(8,128)}, f32[32,40,128]{2,1,0:T(8,128)S(1)}, u32[]{:S(2)}) copy-start(f32[32,40,128]{2,1,0:T(8,128)S(1)} %all-to-all-done.recv) | copy-start | bytes 1966084
  40.3 21.0 %copy-start.6 = (s32[32]{0:T(128)}, s32[32]{0:T(128)S(1)}, u32[]{:S(2)}) copy-start(s32[32]{0:T(128)S(1)} %select_reduce_fusion.place) | copy-start | bytes 388
  41.2 7.0 %collective-permute-start.1 = (f32[4,40,128]{2,1,0:T(8,128)S(1)}, f32[4,40,128]{2,1,0:T(8,128)S(1)}, u32[]{:S(2)}, u32[]{:S(2)}) collective-permute-start(f32[4,40,128]{2,1,0:T(8,128)S(1)} %gather_fusion.2), channel_id=1, source_target_pairs={{8,0},{16,8},{24,16},{9,1},{17,9},{25,17},{10,2},{18,10},{26,18},{... | collective-permute-start | bytes 245768 | tf_op jit(solution)/shard_map/ppermute | solution.py:341
  44.9 7.1 %collective-permute-start = (f32[4,40,128]{2,1,0:T(8,128)S(1)}, f32[4,40,128]{2,1,0:T(8,128)S(1)}, u32[]{:S(2)}, u32[]{:S(2)}) collective-permute-start(f32[4,40,128]{2,1,0:T(8,128)S(1)} %gather_fusion.1), channel_id=1, source_target_pairs={{0,8},{8,16},{16,24},{1,9},{9,17},{17,25},{2,10},{10,18},{18,26},{... | collective-permute-start | bytes 245768 | tf_op jit(solution)/shard_map/ppermute | solution.py:341
  48.2 13.0 %copy-start.3 = (f32[4,40,128]{2,1,0:T(8,128)}, f32[4,40,128]{2,1,0:T(8,128)S(1)}, u32[]{:S(2)}) copy-start(f32[4,40,128]{2,1,0:T(8,128)S(1)} %collective-permute-done.1.bottom) | copy-start | bytes 245764
  52.0 9.3 %copy-start.4 = (f32[4,40,128]{2,1,0:T(8,128)}, f32[4,40,128]{2,1,0:T(8,128)S(1)}, u32[]{:S(2)}) copy-start(f32[4,40,128]{2,1,0:T(8,128)S(1)} %collective-permute-done.top) | copy-start | bytes 245764
  52.0 5.6 %collective-permute-start.2 = (f32[10,40,128]{2,1,0:T(8,128)S(1)}, f32[10,40,128]{2,1,0:T(8,128)S(1)}, u32[]{:S(2)}, u32[]{:S(2)}) collective-permute-start(f32[10,40,128]{2,1,0:T(8,128)S(1)} %pad_maximum_fusion), channel_id=1, source_target_pairs={{0,1},{1,2},{2,3},{3,4},{4,5},{5,6},{6,7},{8,9},{9,10},{10,11},{11... | collective-permute-start | bytes 614408 | tf_op jit(solution)/shard_map/ppermute | solution.py:341
  54.2 7.1 %collective-permute-start.3 = (f32[10,40,128]{2,1,0:T(8,128)S(1)}, f32[10,40,128]{2,1,0:T(8,128)S(1)}, u32[]{:S(2)}, u32[]{:S(2)}) collective-permute-start(f32[10,40,128]{2,1,0:T(8,128)S(1)} %pad_maximum_fusion.1), channel_id=1, source_target_pairs={{1,0},{2,1},{3,2},{4,3},{5,4},{6,5},{7,6},{9,8},{10,9},{11,10},{12... | collective-permute-start | bytes 614408 | tf_op jit(solution)/shard_map/ppermute | solution.py:341
  57.6 3.7 %copy-start.1 = (f32[10,40,128]{2,1,0:T(8,128)}, f32[10,40,128]{2,1,0:T(8,128)S(1)}, u32[]{:S(2)}) copy-start(f32[10,40,128]{2,1,0:T(8,128)S(1)} %collective-permute-done.2.left) | copy-start | bytes 614404
  61.3 0.7 copy-start.2

commit v3 on v2

--- a/solution.py
+++ b/solution.py
@@ -75,8 +75,8 @@
     across = np.kron(np.eye(2), sums_of(HALO)).reshape(2, KF + 1, TILE)
     main = across[:, :KF].reshape(2 * KF, TILE).T
     main = np.concatenate([main] * parts + [np.zeros((TILE, TILE - parts * 2 * KF))], axis=1)
-    extra = np.zeros((rows, TILE))
-    extra[count : count + 2] = across[:, KF]
+    extra = np.zeros((8, TILE))
+    extra[count - rows + 8 : count - rows + 10] = across[:, KF]
     down = np.zeros((rows, raster))
     down[:count] = np.tile(row, (1, parts))
     turned = np.zeros((raster, TILE))
@@ -167,20 +167,34 @@
     row_part = lax.broadcasted_iota(jnp.int32, (raster, TILE), 0) // length
     lane_part = lax.broadcasted_iota(jnp.int32, (raster, TILE), 1) // (2 * KF)
     keep = row_part == lane_part
-    slot_row = lax.broadcasted_iota(jnp.int32, (rows, TILE), 0) == sums + 2
+    last = rows - 8
+    slot_row = lax.broadcasted_iota(jnp.int32, (8, TILE), 0) == sums + 2 - last
     main, extra = (main_hi[...], main_lo[...]), (extra_hi[...], extra_lo[...])
     down, turned = (down_hi[...], down_lo[...]), (turned_hi[...], turned_lo[...])
 
     @pl.loop(0, count // batch)
     def _(i):
+        pixels = jnp.concatenate([strips[order[i * batch + j]] for j in range(batch)], axis=0)
+        pixels = split(transmitted(pixels))
+        wide = dot3(pixels, main)
+        wide = jnp.concatenate(
+            [jnp.where(keep, wide[j * raster : (j + 1) * raster], 0.0) for j in range(batch)],
+            axis=1,
+        )
+        sent = dot3(down, split(wide))
+        turn = dot3(extra, pixels, ((1,), (1,)))
+        turn = jnp.concatenate(
+            [turn[:, j * raster : (j + 1) * raster] for j in range(batch)], axis=0
+        )
+        more = dot3(split(turn), turned)
         for j in range(batch):
             at = i * batch + j
-            pixels = split(transmitted(strips[order[at]]))
-            wide = jnp.where(keep, dot3(pixels, main), 0.0)
-            sent = dot3(down, split(wide))
-            turn = dot3(extra, pixels, ((1,), (1,)))
-            sent = sent + dot3(split(turn), turned)
-            out[at] = jnp.where(slot_row, slots[at], sent)
+            out[at, :last] = sent[:last, j * TILE : (j + 1) * TILE]
+            out[at, last:] = jnp.where(
+                slot_row,
+                slots[at],
+                sent[last:, j * TILE : (j + 1) * TILE] + more[j * 8 : (j + 1) * 8],
+            )
 
 
 def pack(order, slots, strips):
@@ -255,62 +269,69 @@
             sums[at, :TILE] = left[i]
             sums[at, (block_cols + 1) * TILE :] = right[i]
 
-        @pl.loop(0, ext_rows)
-        def _(i):
-            at = pl.ds(pl.multiple_of(i * rows, 8), rows)
-            for j in range(block_cols):
-                tiles = sums[at, j * TILE : (j + 3) * TILE]
-                got = dot3(split(tiles), main)
-                first = kept // 8 * 8
-                ends = jnp.concatenate(
-                    [tiles[first : first + 8, t * TILE : (t + 1) * TILE] for t in range(3)], axis=0
-                )
-                more = dot3(split(ends), extra, ((0,), (0,)))
+        first = kept // 8 * 8
+        for j in range(block_cols):
+            got = dot3(split(sums[:, j * TILE : (j + 3) * TILE]), main)
+            ends = [
+                [
+                    sums[i * rows + first : i * rows + first + 8, t * TILE : (t + 1) * TILE]
+                    for i in range(ext_rows)
+                ]
+                for t in range(j, j + 3)
+            ]
+            ends = jnp.concatenate([jnp.concatenate(e, axis=1) for e in ends], axis=0)
+            more = dot3(split(ends), extra, ((0,), (0,)))
+            for i in range(ext_rows):
                 for p in range(parts):
-                    to = pl.multiple_of((i * parts + p) * rows, 8)
-                    partial[j, pl.ds(to, rows), :] = (
-                        got[:, p * 2 * lanes : (p + 1) * 2 * lanes]
-                        + more[p * 2 * KF : p * 2 * KF + rows]
+                    to, at = (i * parts + p) * rows, i * TILE + p * 2 * KF
+                    partial[j, to : to + rows, :] = (
+                        got[i * rows : (i + 1) * rows, p * 2 * lanes : (p + 1) * 2 * lanes]
+                        + more[at : at + rows]
                     )
 
     first = pl.multiple_of(
         (step * (TILE // length) + edge * parts - HALO // length) * rows, 8
     )
     groups = kern.shape[2] // lanes
+    span = kern.shape[2]
+    part = [partial[j, pl.ds(first, WIN // length * rows), :] for j in range(block_cols)]
+    part = jnp.concatenate(
+        [jnp.concatenate([y[:, ri * lanes : (ri + 1) * lanes] for y in part], axis=1) for ri in (0, 1)],
+        axis=0,
+    )
+    spec = dot3((row_hi[...], row_lo[...]), split(part))
+    prods = []
     for j in range(block_cols):
-        part = partial[j, pl.ds(first, WIN // length * rows), :]
-        part = jnp.concatenate([part[:, :lanes], part[:, lanes:]], axis=0)
-        hi, lo = split(part)
-        spec = mm(row_hi[...], hi) + mm(row_hi[...], lo) + mm(row_lo[...], hi)
-        spec_re = jnp.concatenate([spec[:KF]] * groups, axis=1)
-        spec_im = jnp.concatenate([spec[KF:]] * groups, axis=1)
+        spec_re = jnp.concatenate([spec[:KF, j * lanes : (j + 1) * lanes]] * groups, axis=1)
+        spec_im = jnp.concatenate([spec[KF:, j * lanes : (j + 1) * lanes]] * groups, axis=1)
         prod = jnp.concatenate(
             [kern[0] * spec_re - kern[1] * spec_im, kern[0] * spec_im + kern[1] * spec_re], axis=0
         )
         hi, lo = split(prod)
-        half = mm(up[...], jnp.concatenate([hi, lo, hi], axis=0))
-        half = jnp.concatenate(
-            [
-                jnp.concatenate(
-                    [
-                        half[:COARSE, g * lanes : (g + 1) * lanes],
-                        half[COARSE:, g * lanes : (g + 1) * lanes],
-                    ],
-                    axis=1,
-                )
-                for g in range(groups)
-            ],
-            axis=0,
-        )
-        hi, lo = split(half)
-        field = mm(hi, across_hi[...]) + mm(lo, across_hi[...]) + mm(hi, across_lo[...])
-        wide = field.shape[1] // 2
-        power = field[:, :wide] * field[:, :wide] + field[:, wide:] * field[:, wide:]
-        power = sum(power[g * COARSE : (g + 1) * COARSE] for g in range(groups))
-        hi, lo = split(power)
-        power = mm(hi, wide_hi[...]) + mm(lo, wide_hi[...]) + mm(hi, wide_lo[...])
-        hi, lo = split(power)
-        out[:, j * TILE : (j + 1) * TILE] = mm(fine[...], jnp.concatenate([hi, lo, hi], axis=0))
+        prods.append(jnp.concatenate([hi, lo, hi], axis=0))
+    half = mm(up[...], jnp.concatenate(prods, axis=1))
+    half = jnp.concatenate(
+        [
+            jnp.concatenate(
+                [half[:COARSE, at : at + lanes], half[COARSE:, at : at + lanes]], axis=1
+            )
+            for at in range(0, block_cols * span, lanes)
+        ],
+        axis=0,
+    )
+    field = dot3(split(half), (across_hi[...], across_lo[...]))
+    wide = field.shape[1] // 2
+    power = field[:, :wide] * field[:, :wide] + field[:, wide:] * field[:, wide:]
+    power = [
+        sum(power[(j * groups + g) * COARSE : (j * groups + g + 1) * COARSE] for g in range(groups))
+        for j in range(block_cols)
+    ]
+    power = dot3(split(jnp.concatenate(power, axis=0)), (wide_hi[...], wide_lo[...]))
+    power = jnp.concatenate(
+        [power[j * COARSE : (j + 1) * COARSE] for j in range(block_cols)], axis=1
+    )
+    hi, lo = split(power)
+    out[...] = mm(fine[...], jnp.concatenate([hi, lo, hi], axis=0))
 
 
 def image(raster, place, recv, top, bottom, left, right, kern):

time: 105 us -> 79.8 us (0.76)
  Pallas kernels: 55.2 us -> 30.4 us
    pallas_call x1, Pallas kernels: 42.3 us -> 22.7 us  [image(): pl.pallas_call(functools.partial(image_kernel, raster), grid=(ROWS_DEV //...]
    pallas_call x1, Pallas kernels: 12.9 us -> 7.7 us  [pack(): pl.pallas_call(pack_kernel, in_specs=[smem, smem] + [vmem] * (1 + len(con...]
  transfers between devices with their start and end apart: 5 -> 5, of which waited for: 3 -> 3; matrix products, arithmetic and copies ran while one was open for 3% -> 4% of each run, Pallas kernels for 0% -> 0%
where the time goes in v3:
time: 79.8 us; the launch traced here: 79.5 us
  Pallas kernels  30.4 us (38%)
  waiting for transfers between devices  25.3 us (32%)
  starting transfers between devices  16 us (20%)
  local copies, waits for them, and re-layouts  5.34 us (7%)
  other arithmetic  2.2 us (3%)
    pallas_call x1, Pallas kernels, image(): pl.pallas_call(functools.partial(image_kernel, raster), grid=(ROWS_DEV //...  22.7 us
    all_to_all x1, waiting for transfers between devices, shards(): lax.all_to_all(sent, ('row', 'col'), split_axis=0, concat_axis=0, tiled=T...  17.8 us
    pallas_call x1, Pallas kernels, pack(): pl.pallas_call(pack_kernel, in_specs=[smem, smem] + [vmem] * (1 + len(con...  7.7 us
    all_to_all x1, starting transfers between devices, shards(): lax.all_to_all(sent, ('row', 'col'), split_axis=0, concat_axis=0, tiled=T...  6.38 us
    ppermute x2, starting transfers between devices, swap(): lax.ppermute(low_side, axis, backward)  5.26 us
    ppermute x2, starting transfers between devices, swap(): lax.ppermute(high_side, axis, forward)  4.36 us
    ppermute x2, waiting for transfers between devices, swap(): lax.ppermute(low_side, axis, backward)  3.71 us
    ppermute x2, waiting for transfers between devices, swap(): lax.ppermute(high_side, axis, forward)  3.71 us
  transfers between devices with their start and end apart: 5, of which 3 were waited for; matrix products, arithmetic and copies ran while one was open for 4% of the time, Pallas kernels for 0%

profile of v3, /device:TPU:5, one launch (start us, length us, event | category | flops | bytes accessed | tf_op | source)
XLA Modules:
  0.0 79.5 jit_solution(11211243654394046430)
XLA Ops:
  0.0 0.7 fusion.7
  0.7 0.1 select_reduce_fusion.1.order
  0.8 0.0 copy-start.7
  0.8 1.2 %gather_fusion = f32[32]{0:T(128)} fusion(f32[32]{0:T(128)S(1)} %get-tuple-element.7, s32[1024]{0:T(1024)S(1)} %pad_clamp_fusion.4), kind=kCustom, calls=%fused_computation | custom fusion | bytes 384 | tf_op jit(solution)/shard_map/gather | solution.py:382
  2.0 0.0 copy-done.7
  2.0 0.0 copy-start.5
  2.0 0.0 copy-start.8
  2.0 7.7 %pack.1 = f32[32,40,128]{2,1,0:T(8,128)} custom-call(s32[32]{0:T(128)} %copy-done.7, f32[32]{0:T(128)} %gather_fusion, s32[32,128,128]{2,1,0:T(8,128)} %strips.1, bf16[128,128]{1,0:T(8,128)(2,1)} %constant.118.clone.main_hi, bf16[128,128]{1,0:T(8,128)(2,1)} %constant.119.clone.main_lo, bf16[8,128]{1,0:T(8,128)(2,1)} %constant.120.clone.extra_hi, ...), custom_call_target="tpu_custom_call" | custom-call | tf_op jit(solution)/shard_map/pack/pallas_call | solution.py:204
  9.7 6.4 %all-to-all-start = ((f32[32,40,128]{2,1,0:T(8,128)}), f32[32,40,128]{2,1,0:T(8,128)S(1)}, u32[]{:S(2)}, u32[]{:S(2)}) async-start(f32[32,40,128]{2,1,0:T(8,128)} %pack.1), calls=%async_computation | async-start | bytes 1310720 | tf_op jit(solution)/shard_map/all_to_all | solution.py:383
  16.1 0.0 copy-done.5
  16.1 0.2 reshape.37
  16.4 0.0 copy-done.8
  16.4 17.8 %all-to-all-done.recv = f32[32,40,128]{2,1,0:T(8,128)S(1)} async-done(((f32[32,40,128]{2,1,0:T(8,128)}), f32[32,40,128]{2,1,0:T(8,128)S(1)}, u32[]{:S(2)}, u32[]{:S(2)}) %all-to-all-start) | async-done | bytes 655392 | tf_op jit(solution)/shard_map/all_to_all | solution.py:383
  34.2 0.0 copy-start
  34.2 0.7 fusion.1
  34.9 0.1 select_reduce_fusion.place
  35.0 0.0 copy-start.6
  35.0 0.1 compare_select_fusion.2
  35.1 0.1 reshape.36
  35.2 0.2 fusion.3
  35.4 0.6 gather_fusion.2
  36.0 3.1 %collective-permute-start.1 = (f32[4,40,128]{2,1,0:T(8,128)S(1)}, f32[4,40,128]{2,1,0:T(8,128)S(1)}, u32[]{:S(2)}, u32[]{:S(2)}) collective-permute-start(f32[4,40,128]{2,1,0:T(8,128)S(1)} %gather_fusion.2), channel_id=1, source_target_pairs={{8,0},{16,8},{24,16},{9,1},{17,9},{25,17},{10,2},{18,10},{26,18},{... | collective-permute-start | bytes 245768 | tf_op jit(solution)/shard_map/ppermute | solution.py:362
  39.1 0.6 gather_fusion.1
  39.6 2.2 %collective-permute-start = (f32[4,40,128]{2,1,0:T(8,128)S(1)}, f32[4,40,128]{2,1,0:T(8,128)S(1)}, u32[]{:S(2)}, u32[]{:S(2)}) collective-permute-start(f32[4,40,128]{2,1,0:T(8,128)S(1)} %gather_fusion.1), channel_id=1, source_target_pairs={{0,8},{8,16},{16,24},{1,9},{9,17},{17,25},{2,10},{10,18},{18,26},{... | collective-permute-start | bytes 245768 | tf_op jit(solution)/shard_map/ppermute | solution.py:362
  41.8 0.6 gather_fusion.4
  42.4 0.6 gather_fusion.3
  43.0 0.0 collective-permute-done.1.bottom
  43.0 0.0 copy-start.3
  43.0 3.7 %collective-permute-done.top = f32[4,40,128]{2,1,0:T(8,128)S(1)} collective-permute-done((f32[4,40,128]{2,1,0:T(8,128)S(1)}, f32[4,40,128]{2,1,0:T(8,128)S(1)}, u32[]{:S(2)}, u32[]{:S(2)}) %collective-permute-start) | collective-permute-done | bytes 81952 | tf_op jit(solution)/shard_map/ppermute | solution.py:362
  46.7 0.0 copy-start.4
  46.7 2.2 %collective-permute-start.2 = (f32[10,40,128]{2,1,0:T(8,128)S(1)}, f32[10,40,128]{2,1,0:T(8,128)S(1)}, u32[]{:S(2)}, u32[]{:S(2)}) collective-permute-start(f32[10,40,128]{2,1,0:T(8,128)S(1)} %pad_maximum_fusion), channel_id=1, source_target_pairs={{0,1},{1,2},{2,3},{3,4},{4,5},{5,6},{6,7},{8,9},{9,10},{10,11},{11... | collective-permute-start | bytes 614408 | tf_op jit(solution)/shard_map/ppermute | solution.py:362
  48.9 2.2 %collective-permute-start.3 = (f32[10,40,128]{2,1,0:T(8,128)S(1)}, f32[10,40,128]{2,1,0:T(8,128)S(1)}, u32[]{:S(2)}, u32[]{:S(2)}) collective-permute-start(f32[10,40,128]{2,1,0:T(8,128)S(1)} %pad_maximum_fusion.1), channel_id=1, source_target_pairs={{1,0},{2,1},{3,2},{4,3},{5,4},{6,5},{7,6},{9,8},{10,9},{11,10},{12... | collective-permute-start | bytes 614408 | tf_op jit(solution)/shard_map/ppermute | solution.py:362
  51.1 0.3 fusion
  51.4 0.9 %reshape.38.kern = f32[2,32,512]{2,1,0:T(8,128)} reshape(f32[2,32,16,32]{3,2,1,0:T(8,128)S(1)} %fusion) | data formatting | bytes 262144 | tf_op jit(solution)/shard_map/reshape | solution.py:405
  52.3 0.0 collective-permute-done.2.left
  52.3 0.0 copy-start.1
  52.3 3.7 %collective-permute-done.3.right = f32[10,40,128]{2,1,0:T(8,128)S(1)} collective-permute-done((f32[10,40,128]{2,1,0:T(8,128)S(1)}, f32[10,40,128]{2,1,0:T(8,128)S(1)}, u32[]{:S(2)}, u32[]{:S(2)}) %collective-permute-start.3) | collective-permute-done | bytes 204832 | tf_op jit(solution)/shard_map/ppermute | solution.py:362
  56.0 0.0 copy-done
  56.0 0.0 copy-done.6
  56.0 0.0 copy-done.3
  56.0 0.0 copy-done.4
  56.0 0.0 copy-done.1
  56.0 0.0 copy-start.2
  56.1 0.7 copy-done.2
  56.7 22.7 %image.1 = f32[1024,512]{1,0:T(8,128)} custom-call(s32[32]{0:T(128)} %copy-done.6, f32[32,40,128]{2,1,0:T(8,128)} %copy-done, f32[4,40,128]{2,1,0:T(8,128)} %copy-done.4, f32[4,40,128]{2,1,0:T(8,128)} %copy-done.3, f32[10,40,128]{2,1,0:T(8,128)} %copy-done.1, f32[10,40,128]{2,1,0:T(8,128)} %copy-done.2, f32[2,32,512]{2,1,0:T(8,128)} %reshape.38.kern, ...), custom_call_target="tpu_custom_call" | custom-call | tf_op jit(solution)/shard_map/image/pallas_call | solution.py:344
  (11 shorter events, 0.1 us)
Async XLA Ops:
  0.8 1.2 %copy-start.7 = (s32[32]{0:T(128)}, s32[32]{0:T(128)S(1)}, u32[]{:S(2)}) copy-start(s32[32]{0:T(128)S(1)} %select_reduce_fusion.1.order) | copy-start | bytes 388
  2.0 14.1 %copy-start.5 = (f32[16,2,1024]{2,1,0:T(2,128)S(1)}, f32[16,2,1024]{2,1,0:T(2,128)}, u32[]{:S(2)}) copy-start(f32[16,2,1024]{2,1,0:T(2,128)} %param.26) | copy-start | bytes 393220
  2.0 14.3 %copy-start.8 = (f32[16]{0:T(128)S(1)}, f32[16]{0:T(128)}, u32[]{:S(2)}) copy-start(f32[16]{0:T(128)} %param.27) | copy-start | bytes 196
  9.7 24.5 %all-to-all-start = ((f32[32,40,128]{2,1,0:T(8,128)}), f32[32,40,128]{2,1,0:T(8,128)S(1)}, u32[]{:S(2)}, u32[]{:S(2)}) async-start(f32[32,40,128]{2,1,0:T(8,128)} %pack.1), calls=%async_computation | async-start | bytes 1310720 | tf_op jit(solution)/shard_map/all_to_all | solution.py:383
  34.2 21.8 %copy-start = (f32[32,40,128]{2,1,0:T(8,128)}, f32[32,40,128]{2,1,0:T(8,128)S(1)}, u32[]{:S(2)}) copy-start(f32[32,40,128]{2,1,0:T(8,128)S(1)} %all-to-all-done.recv) | copy-start | bytes 1966084
  35.0 21.0 %copy-start.6 = (s32[32]{0:T(128)}, s32[32]{0:T(128)S(1)}, u32[]{:S(2)}) copy-start(s32[32]{0:T(128)S(1)} %select_reduce_fusion.place) | copy-start | bytes 388
  36.0 7.0 %collective-permute-start.1 = (f32[4,40,128]{2,1,0:T(8,128)S(1)}, f32[4,40,128]{2,1,0:T(8,128)S(1)}, u32[]{:S(2)}, u32[]{:S(2)}) collective-permute-start(f32[4,40,128]{2,1,0:T(8,128)S(1)} %gather_fusion.2), channel_id=1, source_target_pairs={{8,0},{16,8},{24,16},{9,1},{17,9},{25,17},{10,2},{18,10},{26,18},{... | collective-permute-start | bytes 245768 | tf_op jit(solution)/shard_map/ppermute | solution.py:362
  39.6 7.1 %collective-permute-start = (f32[4,40,128]{2,1,0:T(8,128)S(1)}, f32[4,40,128]{2,1,0:T(8,128)S(1)}, u32[]{:S(2)}, u32[]{:S(2)}) collective-permute-start(f32[4,40,128]{2,1,0:T(8,128)S(1)} %gather_fusion.1), channel_id=1, source_target_pairs={{0,8},{8,16},{16,24},{1,9},{9,17},{17,25},{2,10},{10,18},{18,26},{... | collective-permute-start | bytes 245768 | tf_op jit(solution)/shard_map/ppermute | solution.py:362
  43.0 13.0 %copy-start.3 = (f32[4,40,128]{2,1,0:T(8,128)}, f32[4,40,128]{2,1,0:T(8,128)S(1)}, u32[]{:S(2)}) copy-start(f32[4,40,128]{2,1,0:T(8,128)S(1)} %collective-permute-done.1.bottom) | copy-start | bytes 245764
  46.7 9.3 %copy-start.4 = (f32[4,40,128]{2,1,0:T(8,128)}, f32[4,40,128]{2,1,0:T(8,128)S(1)}, u32[]{:S(2)}) copy-start(f32[4,40,128]{2,1,0:T(8,128)S(1)} %collective-permute-done.top) | copy-start | bytes 245764
  46.7 5.6 %collective-permute-start.2 = (f32[10,40,128]{2,1,0:T(8,128)S(1)}, f32[10,40,128]{2,1,0:T(8,128)S(1)}, u32[]{:S(2)}, u32[]{:S(2)}) collective-permute-start(f32[10,40,128]{2,1,0:T(8,128)S(1)} %pad_maximum_fusion), channel_id=1, source_target_pairs={{0,1},{1,2},{2,3},{3,4},{4,5},{5,6},{6,7},{8,9},{9,10},{10,11},{11... | collective-permute-start | bytes 614408 | tf_op jit(solution)/shard_map/ppermute | solution.py:362
  48.9 7.1 %collective-permute-start.3 = (f32[10,40,128]{2,1,0:T(8,128)S(1)}, f32[10,40,128]{2,1,0:T(8,128)S(1)}, u32[]{:S(2)}, u32[]{:S(2)}) collective-permute-start(f32[10,40,128]{2,1,0:T(8,128)S(1)} %pad_maximum_fusion.1), channel_id=1, source_target_pairs={{1,0},{2,1},{3,2},{4,3},{5,4},{6,5},{7,6},{9,8},{10,9},{11,10},{12... | collective-permute-start | bytes 614408 | tf_op jit(solution)/shard_map/ppermute | solution.py:362
  52.3 3.7 %copy-start.1 = (f32[10,40,128]{2,1,0:T(8,128)}, f32[10,40,128]{2,1,0:T(8,128)S(1)}, u32[]{:S(2)}) copy-start(f32[10,40,128]{2,1,0:T(8,128)S(1)} %collective-permute-done.2.left) | copy-start | bytes 614404
  56.0 0.7 copy-start.2

commit v4 on v3

--- a/solution.py
+++ b/solution.py
@@ -146,7 +146,7 @@
 
 
 def pack_kernel(
-    order,
+    owners,
     slots,
     strips,
     main_hi,
@@ -159,11 +159,10 @@
     turned_lo,
     out,
 ):
-    count, rows, _ = out.shape
-    raster = strips.shape[1]
+    rows = out.shape[1]
+    batch, raster, _ = strips.shape
     length = min(raster, HALO)
     sums = sums_of(length).shape[0]
-    batch = math.gcd(count, 8)
     row_part = lax.broadcasted_iota(jnp.int32, (raster, TILE), 0) // length
     lane_part = lax.broadcasted_iota(jnp.int32, (raster, TILE), 1) // (2 * KF)
     keep = row_part == lane_part
@@ -172,42 +171,45 @@
     main, extra = (main_hi[...], main_lo[...]), (extra_hi[...], extra_lo[...])
     down, turned = (down_hi[...], down_lo[...]), (turned_hi[...], turned_lo[...])
 
-    @pl.loop(0, count // batch)
-    def _(i):
-        pixels = jnp.concatenate([strips[order[i * batch + j]] for j in range(batch)], axis=0)
-        pixels = split(transmitted(pixels))
-        wide = dot3(pixels, main)
-        wide = jnp.concatenate(
-            [jnp.where(keep, wide[j * raster : (j + 1) * raster], 0.0) for j in range(batch)],
-            axis=1,
+    pixels = strips[...].reshape(batch * raster, TILE)
+    pixels = split(transmitted(pixels))
+    wide = dot3(pixels, main)
+    wide = jnp.concatenate(
+        [jnp.where(keep, wide[j * raster : (j + 1) * raster], 0.0) for j in range(batch)],
+        axis=1,
+    )
+    sent = dot3(down, split(wide))
+    turn = dot3(extra, pixels, ((1,), (1,)))
+    turn = jnp.concatenate(
+        [turn[:, j * raster : (j + 1) * raster] for j in range(batch)], axis=0
+    )
+    more = dot3(split(turn), turned)
+    for j in range(batch):
+        s = pl.program_id(0) * batch + j
+        at = owners[s]
+        out[at, :last] = sent[:last, j * TILE : (j + 1) * TILE]
+        out[at, last:] = jnp.where(
+            slot_row,
+            slots[s],
+            sent[last:, j * TILE : (j + 1) * TILE] + more[j * 8 : (j + 1) * 8],
         )
-        sent = dot3(down, split(wide))
-        turn = dot3(extra, pixels, ((1,), (1,)))
-        turn = jnp.concatenate(
-            [turn[:, j * raster : (j + 1) * raster] for j in range(batch)], axis=0
-        )
-        more = dot3(split(turn), turned)
-        for j in range(batch):
-            at = i * batch + j
-            out[at, :last] = sent[:last, j * TILE : (j + 1) * TILE]
-            out[at, last:] = jnp.where(
-                slot_row,
-                slots[at],
-                sent[last:, j * TILE : (j + 1) * TILE] + more[j * 8 : (j + 1) * 8],
-            )
-
-
-def pack(order, slots, strips):
+
+
+def pack(owners, slots, strips):
     count, raster, _ = strips.shape
+    rows = sent_rows(min(raster, HALO))
+    batch = math.gcd(count, 8)
     consts = [jnp.asarray(t) for t in pack_tables(raster)]
-    smem, vmem = pl.BlockSpec(memory_space=pltpu.SMEM), pl.BlockSpec(memory_space=pltpu.VMEM)
+    smem = pl.BlockSpec(memory_space=pltpu.SMEM)
     return pl.pallas_call(
         pack_kernel,
-        in_specs=[smem, smem] + [vmem] * (1 + len(consts)),
-        out_specs=vmem,
-        out_shape=jax.ShapeDtypeStruct((count, sent_rows(min(raster, HALO)), TILE), f32),
+        grid=(count // batch,),
+        in_specs=[smem, smem, pl.BlockSpec((batch, raster, TILE), lambda i: (i, 0, 0))]
+        + [pl.BlockSpec(t.shape, lambda i: (0, 0)) for t in consts],
+        out_specs=pl.BlockSpec((count, rows, TILE), lambda i: (0, 0, 0)),
+        out_shape=jax.ShapeDtypeStruct((count, rows, TILE), f32),
         name="pack",
-    )(order, slots, strips, *consts)
+    )(owners, slots, strips, *consts)
 
 
 def image_kernel(
@@ -378,8 +380,7 @@
     strip_col = grid_pos % raster_cols
     owners = strip_row // block_rows * col_count + strip_col // block_cols
     slot_ids = strip_row % block_rows * block_cols + strip_col % block_cols
-    order = inverse(owners)
-    sent = pack(order, slot_ids.astype(f32)[order], strips)
+    sent = pack(owners, slot_ids.astype(f32), strips)
     received = lax.all_to_all(sent, ("row", "col"), split_axis=0, concat_axis=0, tiled=True)
     slot_row = sums_of(min(raster, HALO)).shape[0] + 2
     place = inverse(received[:, slot_row, 0].astype(jnp.int32))

time: 79.8 us -> 79.1 us (level)
  local copies, waits for them, and re-layouts: 5.34 us -> 4.13 us
  other arithmetic: 2.2 us -> 3.21 us
    gather x1 -> x0, local copies, waits for them, and re-layouts: 1.2 us -> none  [shards(): sent = pack(order, slot_ids.astype(f32)[order], strips)]
where the time goes in v4:
time: 79.1 us; the launch traced here: 78.8 us
  Pallas kernels  30 us (38%)
  waiting for transfers between devices  25.3 us (32%)
  starting transfers between devices  16 us (20%)
  local copies, waits for them, and re-layouts  4.13 us (5%)
  other arithmetic  3.21 us (4%)
    pallas_call x1, Pallas kernels, image(): pl.pallas_call(functools.partial(image_kernel, raster), grid=(ROWS_DEV //...  22.7 us
    all_to_all x1, waiting for transfers between devices, shards(): lax.all_to_all(sent, ('row', 'col'), split_axis=0, concat_axis=0, tiled=T...  17.8 us
    pallas_call x1, Pallas kernels, pack(): pl.pallas_call(pack_kernel, grid=(count // batch,), in_specs=[smem, smem,...  7.23 us
    all_to_all x1, starting transfers between devices, shards(): lax.all_to_all(sent, ('row', 'col'), split_axis=0, concat_axis=0, tiled=T...  6.38 us
    ppermute x2, starting transfers between devices, swap(): lax.ppermute(low_side, axis, backward)  5.26 us
    ppermute x2, starting transfers between devices, swap(): lax.ppermute(high_side, axis, forward)  4.36 us
    ppermute x2, waiting for transfers between devices, swap(): lax.ppermute(low_side, axis, backward)  3.72 us
    ppermute x2, waiting for transfers between devices, swap(): lax.ppermute(high_side, axis, forward)  3.71 us
  transfers between devices with their start and end apart: 5, of which 3 were waited for; matrix products, arithmetic and copies ran while one was open for 4% of the time, Pallas kernels for 0%

profile of v4, /device:TPU:5, one launch (start us, length us, event | category | flops | bytes accessed | tf_op | source)
XLA Modules:
  0.0 78.8 jit_solution(10476737684450512268)
XLA Ops:
  0.0 1.3 %fusion.6 = (f32[32]{0:T(128)}, s32[32]{0:T(128)S(1)}, s32[32]{0:T(128)S(1)}, s32[32]{0:T(128)S(1)}) fusion(s32[32]{0:T(128)} %param.25), kind=kLoop, calls=%fused_computation.41 | loop fusion | flops 1408 | bytes 640 | tf_op jit(solution)/shard_map/convert_element_type | solution.py:383
  1.3 0.6 multiply_add_fusion.owners
  1.8 0.0 copy-start.5
  1.8 0.0 copy-start.7
  1.8 7.2 %pack.1 = f32[32,40,128]{2,1,0:T(8,128)} custom-call(s32[32]{0:T(128)} %multiply_add_fusion.owners, f32[32]{0:T(128)} %get-tuple-element.7.slots, s32[32,128,128]{2,1,0:T(8,128)} %strips.1, bf16[128,128]{1,0:T(8,128)(2,1)} %constant.116.clone.main_hi, bf16[128,128]{1,0:T(8,128)(2,1)} %constant.117.clone.main_lo, bf16[8,128]{1,0:T(8,128)(2,1)} %constant.118.clone.extra_hi, ...), custom_call_target="tpu_custom_call" | custom-call | tf_op jit(solution)/shard_map/pack/pallas_call | solution.py:204
  9.1 6.4 %all-to-all-start = ((f32[32,40,128]{2,1,0:T(8,128)}), f32[32,40,128]{2,1,0:T(8,128)S(1)}, u32[]{:S(2)}, u32[]{:S(2)}) async-start(f32[32,40,128]{2,1,0:T(8,128)} %pack.1), calls=%async_computation | async-start | bytes 1310720 | tf_op jit(solution)/shard_map/all_to_all | solution.py:384
  15.4 0.0 copy-done.5
  15.5 0.2 reshape.23
  15.7 0.0 copy-done.7
  15.7 17.8 %all-to-all-done.recv = f32[32,40,128]{2,1,0:T(8,128)S(1)} async-done(((f32[32,40,128]{2,1,0:T(8,128)}), f32[32,40,128]{2,1,0:T(8,128)S(1)}, u32[]{:S(2)}, u32[]{:S(2)}) %all-to-all-start) | async-done | bytes 655392 | tf_op jit(solution)/shard_map/all_to_all | solution.py:384
  33.6 0.0 copy-start
  33.6 0.7 fusion.1
  34.2 0.1 select_reduce_fusion.place
  34.3 0.0 copy-start.6
  34.4 0.1 compare_select_fusion.2
  34.4 0.1 reshape.22
  34.5 0.2 fusion.3
  34.7 0.6 gather_fusion.1
  35.3 3.1 %collective-permute-start.1 = (f32[4,40,128]{2,1,0:T(8,128)S(1)}, f32[4,40,128]{2,1,0:T(8,128)S(1)}, u32[]{:S(2)}, u32[]{:S(2)}) collective-permute-start(f32[4,40,128]{2,1,0:T(8,128)S(1)} %gather_fusion.1), channel_id=1, source_target_pairs={{8,0},{16,8},{24,16},{9,1},{17,9},{25,17},{10,2},{18,10},{26,18},{... | collective-permute-start | bytes 245768 | tf_op jit(solution)/shard_map/ppermute | solution.py:364
  38.4 0.6 gather_fusion
  38.9 2.2 %collective-permute-start = (f32[4,40,128]{2,1,0:T(8,128)S(1)}, f32[4,40,128]{2,1,0:T(8,128)S(1)}, u32[]{:S(2)}, u32[]{:S(2)}) collective-permute-start(f32[4,40,128]{2,1,0:T(8,128)S(1)} %gather_fusion), channel_id=1, source_target_pairs={{0,8},{8,16},{16,24},{1,9},{9,17},{17,25},{2,10},{10,18},{18,26},{... | collective-permute-start | bytes 245768 | tf_op jit(solution)/shard_map/ppermute | solution.py:364
  41.2 0.6 gather_fusion.3
  41.7 0.6 gather_fusion.2
  42.3 0.0 collective-permute-done.1.bottom
  42.3 0.0 copy-start.3
  42.3 3.7 %collective-permute-done.top = f32[4,40,128]{2,1,0:T(8,128)S(1)} collective-permute-done((f32[4,40,128]{2,1,0:T(8,128)S(1)}, f32[4,40,128]{2,1,0:T(8,128)S(1)}, u32[]{:S(2)}, u32[]{:S(2)}) %collective-permute-start) | collective-permute-done | bytes 81952 | tf_op jit(solution)/shard_map/ppermute | solution.py:364
  46.0 0.0 copy-start.4
  46.1 2.2 %collective-permute-start.2 = (f32[10,40,128]{2,1,0:T(8,128)S(1)}, f32[10,40,128]{2,1,0:T(8,128)S(1)}, u32[]{:S(2)}, u32[]{:S(2)}) collective-permute-start(f32[10,40,128]{2,1,0:T(8,128)S(1)} %pad_maximum_fusion), channel_id=1, source_target_pairs={{0,1},{1,2},{2,3},{3,4},{4,5},{5,6},{6,7},{8,9},{9,10},{10,11},{11... | collective-permute-start | bytes 614408 | tf_op jit(solution)/shard_map/ppermute | solution.py:364
  48.3 2.2 %collective-permute-start.3 = (f32[10,40,128]{2,1,0:T(8,128)S(1)}, f32[10,40,128]{2,1,0:T(8,128)S(1)}, u32[]{:S(2)}, u32[]{:S(2)}) collective-permute-start(f32[10,40,128]{2,1,0:T(8,128)S(1)} %pad_maximum_fusion.1), channel_id=1, source_target_pairs={{1,0},{2,1},{3,2},{4,3},{5,4},{6,5},{7,6},{9,8},{10,9},{11,10},{12... | collective-permute-start | bytes 614408 | tf_op jit(solution)/shard_map/ppermute | solution.py:364
  50.4 0.3 fusion
  50.7 0.9 %reshape.24.kern = f32[2,32,512]{2,1,0:T(8,128)} reshape(f32[2,32,16,32]{3,2,1,0:T(8,128)S(1)} %fusion) | data formatting | bytes 262144 | tf_op jit(solution)/shard_map/reshape | solution.py:406
  51.6 0.0 collective-permute-done.2.left
  51.6 0.0 copy-start.1
  51.6 3.7 %collective-permute-done.3.right = f32[10,40,128]{2,1,0:T(8,128)S(1)} collective-permute-done((f32[10,40,128]{2,1,0:T(8,128)S(1)}, f32[10,40,128]{2,1,0:T(8,128)S(1)}, u32[]{:S(2)}, u32[]{:S(2)}) %collective-permute-start.3) | collective-permute-done | bytes 204832 | tf_op jit(solution)/shard_map/ppermute | solution.py:364
  55.3 0.0 copy-done
  55.3 0.0 copy-done.6
  55.3 0.0 copy-done.3
  55.3 0.0 copy-done.4
  55.3 0.0 copy-done.1
  55.4 0.0 copy-start.2
  55.4 0.7 copy-done.2
  56.0 22.7 %image.1 = f32[1024,512]{1,0:T(8,128)} custom-call(s32[32]{0:T(128)} %copy-done.6, f32[32,40,128]{2,1,0:T(8,128)} %copy-done, f32[4,40,128]{2,1,0:T(8,128)} %copy-done.4, f32[4,40,128]{2,1,0:T(8,128)} %copy-done.3, f32[10,40,128]{2,1,0:T(8,128)} %copy-done.1, f32[10,40,128]{2,1,0:T(8,128)} %copy-done.2, f32[2,32,512]{2,1,0:T(8,128)} %reshape.24.kern, ...), custom_call_target="tpu_custom_call" | custom-call | tf_op jit(solution)/shard_map/image/pallas_call | solution.py:346
  (8 shorter events, 0.1 us)
Async XLA Ops:
  1.8 13.6 %copy-start.5 = (f32[16,2,1024]{2,1,0:T(2,128)S(1)}, f32[16,2,1024]{2,1,0:T(2,128)}, u32[]{:S(2)}) copy-start(f32[16,2,1024]{2,1,0:T(2,128)} %param.26) | copy-start | bytes 393220
  1.8 13.9 %copy-start.7 = (f32[16]{0:T(128)S(1)}, f32[16]{0:T(128)}, u32[]{:S(2)}) copy-start(f32[16]{0:T(128)} %param.27) | copy-start | bytes 196
  9.1 24.5 %all-to-all-start = ((f32[32,40,128]{2,1,0:T(8,128)}), f32[32,40,128]{2,1,0:T(8,128)S(1)}, u32[]{:S(2)}, u32[]{:S(2)}) async-start(f32[32,40,128]{2,1,0:T(8,128)} %pack.1), calls=%async_computation | async-start | bytes 1310720 | tf_op jit(solution)/shard_map/all_to_all | solution.py:384
  33.6 21.8 %copy-start = (f32[32,40,128]{2,1,0:T(8,128)}, f32[32,40,128]{2,1,0:T(8,128)S(1)}, u32[]{:S(2)}) copy-start(f32[32,40,128]{2,1,0:T(8,128)S(1)} %all-to-all-done.recv) | copy-start | bytes 1966084
  34.3 21.0 %copy-start.6 = (s32[32]{0:T(128)}, s32[32]{0:T(128)S(1)}, u32[]{:S(2)}) copy-start(s32[32]{0:T(128)S(1)} %select_reduce_fusion.place) | copy-start | bytes 388
  35.3 7.0 %collective-permute-start.1 = (f32[4,40,128]{2,1,0:T(8,128)S(1)}, f32[4,40,128]{2,1,0:T(8,128)S(1)}, u32[]{:S(2)}, u32[]{:S(2)}) collective-permute-start(f32[4,40,128]{2,1,0:T(8,128)S(1)} %gather_fusion.1), channel_id=1, source_target_pairs={{8,0},{16,8},{24,16},{9,1},{17,9},{25,17},{10,2},{18,10},{26,18},{... | collective-permute-start | bytes 245768 | tf_op jit(solution)/shard_map/ppermute | solution.py:364
  38.9 7.1 %collective-permute-start = (f32[4,40,128]{2,1,0:T(8,128)S(1)}, f32[4,40,128]{2,1,0:T(8,128)S(1)}, u32[]{:S(2)}, u32[]{:S(2)}) collective-permute-start(f32[4,40,128]{2,1,0:T(8,128)S(1)} %gather_fusion), channel_id=1, source_target_pairs={{0,8},{8,16},{16,24},{1,9},{9,17},{17,25},{2,10},{10,18},{18,26},{... | collective-permute-start | bytes 245768 | tf_op jit(solution)/shard_map/ppermute | solution.py:364
  42.3 13.0 %copy-start.3 = (f32[4,40,128]{2,1,0:T(8,128)}, f32[4,40,128]{2,1,0:T(8,128)S(1)}, u32[]{:S(2)}) copy-start(f32[4,40,128]{2,1,0:T(8,128)S(1)} %collective-permute-done.1.bottom) | copy-start | bytes 245764
  46.0 9.3 %copy-start.4 = (f32[4,40,128]{2,1,0:T(8,128)}, f32[4,40,128]{2,1,0:T(8,128)S(1)}, u32[]{:S(2)}) copy-start(f32[4,40,128]{2,1,0:T(8,128)S(1)} %collective-permute-done.top) | copy-start | bytes 245764
  46.1 5.6 %collective-permute-start.2 = (f32[10,40,128]{2,1,0:T(8,128)S(1)}, f32[10,40,128]{2,1,0:T(8,128)S(1)}, u32[]{:S(2)}, u32[]{:S(2)}) collective-permute-start(f32[10,40,128]{2,1,0:T(8,128)S(1)} %pad_maximum_fusion), channel_id=1, source_target_pairs={{0,1},{1,2},{2,3},{3,4},{4,5},{5,6},{6,7},{8,9},{9,10},{10,11},{11... | collective-permute-start | bytes 614408 | tf_op jit(solution)/shard_map/ppermute | solution.py:364
  48.3 7.1 %collective-permute-start.3 = (f32[10,40,128]{2,1,0:T(8,128)S(1)}, f32[10,40,128]{2,1,0:T(8,128)S(1)}, u32[]{:S(2)}, u32[]{:S(2)}) collective-permute-start(f32[10,40,128]{2,1,0:T(8,128)S(1)} %pad_maximum_fusion.1), channel_id=1, source_target_pairs={{1,0},{2,1},{3,2},{4,3},{5,4},{6,5},{7,6},{9,8},{10,9},{11,10},{12... | collective-permute-start | bytes 614408 | tf_op jit(solution)/shard_map/ppermute | solution.py:364
  51.6 3.7 %copy-start.1 = (f32[10,40,128]{2,1,0:T(8,128)}, f32[10,40,128]{2,1,0:T(8,128)S(1)}, u32[]{:S(2)}) copy-start(f32[10,40,128]{2,1,0:T(8,128)S(1)} %collective-permute-done.2.left) | copy-start | bytes 614404
  55.4 0.7 copy-start.2
